TPU v7x, 512 devices: a whole 4x4x16 slice. The times are simulated.
512 devices in a mesh: dp: 32 (over y, x, core), tensor: 16 (over z).
Axes of the slice: x: 4, y: 4, z: 16, core: 2. Of those that a mesh axis runs over, the one named last changes fastest.
Arguments:
- tokens: bfloat16 [16384, 8192], P('dp', 'tensor'), may hold values from -6 to 6
- out_grad: bfloat16 [16384, 28672], P('dp', 'tensor'), may hold values from -6 to 6
- galore_basis: bfloat16 [8192, 512], P('tensor'), may hold values from -0.0625 to 0.0625
- first_moment: float32 [512, 28672], P('dp', 'tensor'), may hold values from -4 to 4
- second_moment: float32 [512, 28672], P('dp', 'tensor'), may hold values from 0.05 to 5
- list_lengths: int32 [128], P('dp'), may hold values from 1 to 128, as said below
Outputs:
- new_first: float32 [512, 28672], P('dp', 'tensor')
- new_second: float32 [512, 28672], P('dp', 'tensor')
- weight_step: bfloat16 [8192, 28672], P('dp', 'tensor')
Inputs may be any that keep to these rules, and one draw needn't show every extreme that they name: `list_lengths`: live slots of a list come first in its 128 slots.
All inputs are finite; a program needn't handle non-finite values.
Results may differ from a plain program's by a relative error of at most 0.0051.
Values may be sent and summed in bfloat16 or wider, within the bound.
No kernel may reach another device: no remote copies, remote signals or barrier semaphores. Data moves between devices by JAX's collectives and lax.ppermute only.
A program may use at most 64 MiB of HBM per device.

v0:
```python
import jax
import jax.numpy as jnp
from jax import lax
from jax.sharding import PartitionSpec as P

SLOTS = 128
STEP = 1000


beta_first = 0.9
beta_second = 0.999
epsilon = 1e-08


def in_blocks(x, dim, peers):
    dims = x.shape
    tiles = x.reshape(*dims[:dim], peers, dims[dim] // peers, *dims[dim + 1 :])
    return jnp.moveaxis(tiles, dim, 0)


def summed_on_arrival(x, axis, dim):
    tiles = in_blocks(x, dim, lax.axis_size(axis))
    arrived = lax.all_to_all(tiles, axis, split_axis=0, concat_axis=0, tiled=True)
    return arrived.sum(axis=0)


def broadcast(x, axis, root):
    return lax.dynamic_index_in_dim(lax.all_gather(x, axis), root, 0, keepdims=False)


def copy_for_each(x, axis):
    copies = jnp.broadcast_to(x, (lax.axis_size(axis), *x.shape))
    return lax.all_to_all(copies, axis, split_axis=0, concat_axis=0, tiled=True)


def in_order(tiles, dim):
    tiles = jnp.moveaxis(tiles, 0, dim)
    dims = tiles.shape
    return tiles.reshape(*dims[:dim], dims[dim] * dims[dim + 1], *dims[dim + 2 :])


def gather_directly(x, axis, dim):
    tiles = copy_for_each(x, axis)
    return in_order(tiles, dim)


def token_weights(list_lengths):
    slot_index = jnp.arange(SLOTS, dtype=jnp.int32)
    live_slots = slot_index[None, :] < list_lengths[:, None]
    scaled = jnp.where(
        live_slots, 1.0 / list_lengths[:, None].astype(jnp.float32), jnp.float32(0.0)
    )
    return scaled.reshape(-1)


def body(tokens, out_grad, galore_basis, first_moment, second_moment, list_lengths):
    partial_coords = jnp.dot(tokens, galore_basis, preferred_element_type=jnp.float32)
    coordinates = lax.psum(partial_coords, "tensor")
    weighted = (coordinates * token_weights(list_lengths)[:, None]).astype(jnp.bfloat16)
    gradient = summed_on_arrival(
        lax.dot_general(
            weighted, out_grad, (((0,), (0,)), ((), ())), preferred_element_type=jnp.float32
        ),
        "dp",
        0,
    )
    new_first = beta_first * first_moment + (1.0 - beta_first) * gradient
    new_second = beta_second * second_moment + (1.0 - beta_second) * gradient * gradient
    corrected_first = new_first / (1.0 - beta_first**STEP)
    corrected_second = new_second / (1.0 - beta_second**STEP)
    update = (corrected_first / (jnp.sqrt(corrected_second) + epsilon)).astype(jnp.bfloat16)
    replicas = lax.axis_size("dp")
    splits = lax.axis_size("tensor")
    block_rows = galore_basis.shape[0] * splits // replicas
    replica = lax.axis_index("dp")
    group_ratio = replicas // splits
    holder = broadcast(galore_basis, "tensor", replica // group_ratio)
    local_basis = lax.dynamic_slice_in_dim(
        holder, replica % group_ratio * block_rows, block_rows, 0
    )
    initial = jnp.zeros((block_rows, update.shape[1]), jnp.float32)
    segment = gather_directly(update, "dp", 0)
    factor = lax.slice_in_dim(local_basis, 0, segment.shape[0], axis=1)
    expanded = initial + jnp.dot(factor, segment, preferred_element_type=jnp.float32)
    weight_step = (-expanded).astype(jnp.bfloat16)
    return (new_first, new_second, weight_step)


def solution(mesh):
    in_specs = (
        P("dp", "tensor"),
        P("dp", "tensor"),
        P("tensor", None),
        P("dp", "tensor"),
        P("dp", "tensor"),
        P("dp"),
    )
    out_specs = (P("dp", "tensor"), P("dp", "tensor"), P("dp", "tensor"))
    return jax.shard_map(body, mesh=mesh, in_specs=in_specs, out_specs=out_specs, check_vma=False)
```

profile of v0, /device:TPU:1, one launch (start us, length us, event | category | flops | bytes accessed | tf_op | source)
XLA Modules:
  0.0 269.2 jit_solution(6594437257509538033)
XLA Ops:
  7.2 0.0 copy-start
  7.2 0.0 copy-start.3
  7.2 0.0 all-reduce.2.cloned.1.call-start
  7.2 2.7 %fusion.8 = f32[512,512]{1,0:T(8,128)} fusion(bf16[512,512]{1,0:T(8,128)(2,1)} %param.6, bf16[512,512]{1,0:T(8,128)(2,1)} %param.8), kind=kOutput, calls=%fused_computation.15 | convolution fusion | flops 268435456 | bytes 2097152 | tf_op jit(solution)/shard_map/dot_general | solution.py:57
  10.0 0.0 all-reduce.2.cloned.1.call-update
  10.0 0.0 all-gather.3.cloned.1.call-start
  10.0 0.7 all-gather.3.cloned.1.call-update
  10.7 0.0 copy-done.3
  10.8 0.1 select_bitcast_fusion
  10.8 134.3 %all-reduce.2.cloned.1.call-done = f32[512,512]{1,0:T(8,128)} async-done(((f32[512,512]{1,0:T(8,128)}), f32[512,512]{1,0:T(8,128)}) %all-reduce.2.cloned.1.call-update) | async-done | bytes 1048592 | tf_op jit(solution)/shard_map/psum | solution.py:58
  145.1 0.0 copy-done
  145.1 2.5 fusion.1
  147.6 62.2 %all_to_all.10 = f32[32,16,1792]{2,1,0:T(8,128)} all-to-all(f32[32,16,1792]{2,1,0:T(8,128)S(1)} %bitcast.12), channel_id=1, replica_groups=mesh['dp'=32,'tensor'=16] {'dp'}, dimensions={0} | all-to-all | bytes 7340032 | tf_op jit(solution)/shard_map/all_to_all | solution.py:23
  209.8 0.0 copy-start.1
  209.8 0.0 copy-start.2
  209.8 2.3 reduce_sum.9
  212.1 0.0 copy-done.1
  212.1 0.0 copy-done.2
  212.1 0.7 divide_convert_fusion
  212.9 1.3 broadcast_in_dim.20
  214.2 4.7 %all-to-all-start.1 = ((bf16[32,16,1792]{2,1,0:T(8,128)(2,1)}), bf16[32,16,1792]{2,1,0:T(8,128)(2,1)}, u32[]{:S(2)}, u32[]{:S(2)}) async-start(bf16[32,16,1792]{2,1,0:T(8,128)(2,1)} %broadcast_in_dim.20), calls=%async_computation.1 | async-start | bytes 3670016 | tf_op jit(solution)/shard_map/all_to_all | solution.py:33
  219.0 25.8 %all-to-all-done.1 = bf16[32,16,1792]{2,1,0:T(8,128)(2,1)} async-done(((bf16[32,16,1792]{2,1,0:T(8,128)(2,1)}), bf16[32,16,1792]{2,1,0:T(8,128)(2,1)}, u32[]{:S(2)}, u32[]{:S(2)}) %all-to-all-start.1) | async-done | bytes 1835040 | tf_op jit(solution)/shard_map/all_to_all | solution.py:33
  244.7 14.5 %all-gather.3.cloned.1.call-done = bf16[8192,512]{1,0:T(8,128)(2,1)} async-done(((bf16[512,512]{1,0:T(8,128)(2,1)}), bf16[8192,512]{1,0:T(8,128)(2,1)}) %all-gather.3.cloned.1.call-update) | async-done | bytes 8388624 | tf_op jit(solution)/shard_map/all_gather | solution.py:28
  259.2 3.2 %fusion = bf16[256,1792]{1,0:T(8,128)(2,1)} fusion(bf16[512,1792]{1,0:T(8,128)(2,1)} %bitcast.4, bf16[16,512,512]{2,1,0:T(8,128)(2,1)} %bitcast.13, s32[]{:T(128)S(6)} %select_n.37, s32[]{:T(128)S(6)} %select_n.40), kind=kOutput, calls=%fused_computation.1 | convolution fusion | flops 470679552 | bytes 3014664 | tf_op jit(solution)/shard_map/dot_general | solution.py:84
  (1 shorter events, 0.0 us)
Async XLA Ops:
  7.2 137.9 %copy-start = (bf16[512,1792]{1,0:T(8,128)(2,1)S(1)}, bf16[512,1792]{1,0:T(8,128)(2,1)}, u32[]{:S(2)}) copy-start(bf16[512,1792]{1,0:T(8,128)(2,1)} %param.7) | copy-start | bytes 5505028
  7.2 3.6 %copy-start.3 = (s32[4]{0:T(128)S(1)}, s32[4]{0:T(128)}, u32[]{:S(2)}) copy-start(s32[4]{0:T(128)} %param.11) | copy-start | bytes 52
  7.2 137.9 %all-reduce.2.cloned.1.call-start = ((), (), s32[]{:S(2)}) async-start(), calls=%async_computation.2 | async-start | bytes 2097152 | tf_op jit(solution)/shard_map/psum | solution.py:58
  10.0 249.2 %all-gather.3.cloned.1.call-start = ((), (), s32[]{:S(2)}) async-start(), calls=%async_computation.3 | async-start | bytes 8912896 | tf_op jit(solution)/shard_map/all_gather | solution.py:28
  209.8 2.3 copy-start.1
  209.8 2.3 copy-start.2
  214.2 30.5 %all-to-all-start.1 = ((bf16[32,16,1792]{2,1,0:T(8,128)(2,1)}), bf16[32,16,1792]{2,1,0:T(8,128)(2,1)}, u32[]{:S(2)}, u32[]{:S(2)}) async-start(bf16[32,16,1792]{2,1,0:T(8,128)(2,1)} %broadcast_in_dim.20), calls=%async_computation.1 | async-start | bytes 3670016 | tf_op jit(solution)/shard_map/all_to_all | solution.py:33
Sparse Core Ops, SparseCore 0:
  10.3 134.7 all-reduce.1
  147.2 111.9 all-gather.2
where the time goes:
time: 270 us; the launch traced here: 269 us
  waiting for transfers between devices  175 us (65%)
  blocking collectives  62.2 us (23%)
  between operations  14.1 us (5%)
  matrix products  8.34 us (3%)
  starting transfers between devices  4.8 us (2%)
  other arithmetic  3.12 us (1%)
    psum x1, waiting for transfers between devices, body(): coordinates = lax.psum(partial_coords, 'tensor')  134 us
    all_to_all x1, blocking collectives, summed_on_arrival(): lax.all_to_all(tiles, axis, split_axis=0, concat_axis=0, tiled=True)  62.2 us
    all_to_all x1, waiting for transfers between devices, copy_for_each(): return lax.all_to_all(copies, axis, split_axis=0, concat_axis=0, tiled=True)  25.8 us
    all_gather x1, waiting for transfers between devices, broadcast(): lax.all_gather(x, axis)  14.5 us
  transfers between devices with their start and end apart: 3, of which 3 were waited for; matrix products, arithmetic and copies ran while one was open for 3% of the time, Pallas kernels for 0%

commit v1 on v0

v1 whole, which is shorter than its diff:
```python
import jax
import jax.numpy as jnp
from jax import lax
from jax.sharding import PartitionSpec as P

SLOTS = 128
STEP = 1000


beta_first = 0.9
beta_second = 0.999
epsilon = 1e-08

bf16 = jnp.bfloat16
f32 = jnp.float32


def exchange(tiles, axis, groups=None):
    return lax.all_to_all(tiles, axis, split_axis=0, concat_axis=0, tiled=True, axis_index_groups=groups)


def copies_to_all(x, axis, peers, groups=None):
    return exchange(jnp.broadcast_to(x, (peers, *x.shape)), axis, groups)


def token_weights(list_lengths):
    slot_index = jnp.arange(SLOTS, dtype=jnp.int32)
    live_slots = slot_index[None, :] < list_lengths[:, None]
    scaled = jnp.where(
        live_slots, 1.0 / list_lengths[:, None].astype(jnp.float32), jnp.float32(0.0)
    )
    return scaled.reshape(-1)


def basis_routes(chips, splits):
    return [
        ((2 * k + b) * splits + s, (2 * s + b) * splits + (k - s) % splits)
        for k in range(chips)
        for b in range(2)
        for s in range(splits)
    ]


def body(tokens, out_grad, galore_basis, first_moment, second_moment, list_lengths):
    replicas = lax.axis_size("dp")
    splits = lax.axis_size("tensor")
    chips = replicas // 2
    replica = lax.axis_index("dp")
    core = replica % 2
    rank = galore_basis.shape[1]
    owned = rank // replicas
    columns = out_grad.shape[1]
    slots = tokens.shape[0]
    same_core = [[2 * i + c for i in range(chips)] for c in range(2)]
    partner = [(i, i ^ 1) for i in range(replicas)]

    block_rows = galore_basis.shape[0] * splits // replicas
    half_block = lax.dynamic_slice_in_dim(galore_basis, core * block_rows, block_rows, 0)
    local_basis = lax.ppermute(half_block, ("dp", "tensor"), basis_routes(chips, splits))

    partial = lax.dot_general(
        galore_basis, tokens, (((0,), (1,)), ((), ())), preferred_element_type=f32
    ).astype(bf16)
    arrived = exchange(partial.reshape(splits, rank // splits, slots), "tensor")
    coordinates = arrived.astype(f32).sum(axis=0)
    weighted = (coordinates * token_weights(list_lengths)[None, :]).astype(bf16)
    weighted = lax.all_gather(weighted, "tensor", axis=0, tiled=True)
    by_owner = weighted.reshape(chips, 2, owned, slots)
    other = lax.dynamic_index_in_dim(by_owner, 1 - core, 1, keepdims=False).reshape(rank // 2, slots)
    own = lax.dynamic_index_in_dim(by_owner, core, 1, keepdims=False).reshape(rank // 2, slots)
    sent = jnp.dot(other, out_grad, preferred_element_type=f32).astype(bf16)
    received = lax.ppermute(sent, "dp", partner)
    kept = jnp.dot(own, out_grad, preferred_element_type=f32)
    chip_sum = (kept + received.astype(f32)).astype(bf16).reshape(chips, owned, columns)
    gradient = exchange(chip_sum, "dp", same_core).astype(f32).sum(axis=0)

    new_first = beta_first * first_moment + (1.0 - beta_first) * gradient
    new_second = beta_second * second_moment + (1.0 - beta_second) * gradient * gradient
    corrected_first = new_first / (1.0 - beta_first**STEP)
    corrected_second = new_second / (1.0 - beta_second**STEP)
    update = (corrected_first / (jnp.sqrt(corrected_second) + epsilon)).astype(bf16)

    own_rows = copies_to_all(update, "dp", chips, same_core).reshape(rank // 2, columns)
    other_rows = lax.ppermute(own_rows, "dp", partner)
    place = jnp.arange(rank, dtype=jnp.int32)
    side = place // (rank // 2)
    within = place % (rank // 2)
    source = (within // owned) * (2 * owned) + jnp.where(side == 0, core, 1 - core) * owned + within % owned
    pick = (place[:, None] == source[None, :]).astype(bf16)
    ordered = jnp.dot(local_basis, pick, preferred_element_type=f32).astype(bf16)
    expanded = jnp.dot(ordered[:, : rank // 2], own_rows, preferred_element_type=f32)
    expanded = expanded + jnp.dot(ordered[:, rank // 2 :], other_rows, preferred_element_type=f32)
    weight_step = (-expanded).astype(bf16)
    return (new_first, new_second, weight_step)


def solution(mesh):
    in_specs = (
        P("dp", "tensor"),
        P("dp", "tensor"),
        P("tensor", None),
        P("dp", "tensor"),
        P("dp", "tensor"),
        P("dp"),
    )
    out_specs = (P("dp", "tensor"), P("dp", "tensor"), P("dp", "tensor"))
    return jax.shard_map(body, mesh=mesh, in_specs=in_specs, out_specs=out_specs, check_vma=False)
```

time: 270 us -> 161 us (0.60)
  the two profiles are of different devices: /device:TPU:1 before, /device:TPU:62 now
where the time goes in v1:
time: 161 us
  blocking collectives  68 us (42%)
  waiting for transfers between devices  56.3 us (35%)
  starting transfers between devices  27.3 us (17%)
  matrix products  7.21 us (4%)
    all_to_all x2, blocking collectives, exchange(): lax.all_to_all(tiles, axis, split_axis=0, concat_axis=0, tiled=True, axis...  37.3 us
    all_gather x1, blocking collectives, body(): weighted = lax.all_gather(weighted, 'tensor', axis=0, tiled=True)  30.8 us
    all_to_all x1, waiting for transfers between devices, exchange(): lax.all_to_all(tiles, axis, split_axis=0, concat_axis=0, tiled=True, axis...  28.4 us
    ppermute x1, waiting for transfers between devices, body(): lax.ppermute(half_block, ('dp', 'tensor'), basis_routes(chips, splits))  25.5 us
    all_to_all x1, starting transfers between devices, exchange(): lax.all_to_all(tiles, axis, split_axis=0, concat_axis=0, tiled=True, axis...  15.2 us
    ppermute x1, starting transfers between devices, body(): lax.ppermute(half_block, ('dp', 'tensor'), basis_routes(chips, splits))  8.29 us
  transfers between devices with their start and end apart: 4, of which 3 were waited for; matrix products, arithmetic and copies ran while one was open for 1% of the time, Pallas kernels for 0%

profile of v1, /device:TPU:62, one launch (start us, length us, event | category | flops | bytes accessed | tf_op | source)
XLA Modules:
  0.0 160.9 jit_solution(582919417251868514)
XLA Ops:
  0.6 0.0 copy-start
  0.6 0.0 copy-start.4
  0.7 2.6 %convolution_convert_fusion.1 = bf16[512,512]{1,0:T(8,128)(2,1)} fusion(bf16[512,512]{1,0:T(8,128)(2,1)} %param.8, bf16[512,512]{1,0:T(8,128)(2,1)} %param.6), kind=kOutput, calls=%fused_computation.6 | convolution fusion | flops 268697600 | bytes 1572864 | tf_op jit(solution)/shard_map/dot_general | solution.py:61
  3.3 15.2 %all-to-all-start = ((bf16[16,32,512]{2,1,0:T(8,128)(2,1)}), bf16[16,32,512]{2,1,0:T(8,128)(2,1)S(1)}, u32[]{:S(2)}, u32[]{:S(2)}) async-start(bf16[16,32,512]{2,1,0:T(8,128)(2,1)} %bitcast), calls=%async_computation | async-start | bytes 1048576 | tf_op jit(solution)/shard_map/all_to_all | solution.py:19
  18.5 0.0 copy-done.4
  18.5 0.1 select_bitcast_fusion
  18.6 28.4 %all-to-all-done = bf16[16,32,512]{2,1,0:T(8,128)(2,1)S(1)} async-done(((bf16[16,32,512]{2,1,0:T(8,128)(2,1)}), bf16[16,32,512]{2,1,0:T(8,128)(2,1)S(1)}, u32[]{:S(2)}, u32[]{:S(2)}) %all-to-all-start) | async-done | bytes 524320 | tf_op jit(solution)/shard_map/all_to_all | solution.py:19
  47.0 0.1 convert_reduce_fusion.1
  47.1 30.8 %all_gather.3 = bf16[512,512]{1,0:T(8,128)(2,1)S(1)} all-gather(bf16[32,512]{1,0:T(8,128)(2,1)S(1)} %multiply_convert_fusion), channel_id=1, replica_groups=mesh['dp'=32,'tensor'=16] {'tensor'}, dimensions={0}, use_global_device_ids=true | all-gather | bytes 557056 | tf_op jit(solution)/shard_map/all_gather | solution.py:67
  77.9 0.0 copy-done
  77.9 0.6 convolution_convert_fusion
  78.5 1.9 %collective-permute-start = (bf16[256,1792]{1,0:T(8,128)(2,1)S(1)}, bf16[256,1792]{1,0:T(8,128)(2,1)S(1)}, u32[]{:S(2)}, u32[]{:S(2)}) collective-permute-start(bf16[256,1792]{1,0:T(8,128)(2,1)S(1)} %convolution_convert_fusion), channel_id=1, source_target_pairs={{0,16},{16,0},{32,48},{48,32},{64,80},{80,64},{96,112},{112,96},{1... | collective-permute-start | bytes 2752520 | tf_op jit(solution)/shard_map/ppermute | solution.py:72
  80.5 2.4 %collective-permute-done = bf16[256,1792]{1,0:T(8,128)(2,1)S(1)} collective-permute-done((bf16[256,1792]{1,0:T(8,128)(2,1)S(1)}, bf16[256,1792]{1,0:T(8,128)(2,1)S(1)}, u32[]{:S(2)}, u32[]{:S(2)}) %collective-permute-start) | collective-permute-done | bytes 917536 | tf_op jit(solution)/shard_map/ppermute | solution.py:72
  82.9 0.6 add_convert_fusion
  83.5 0.0 copy-start.2
  83.6 0.0 copy-start.3
  83.6 19.0 %all_to_all.15 = bf16[16,16,1792]{2,1,0:T(8,128)(2,1)S(1)} all-to-all(bf16[16,16,1792]{2,1,0:T(8,128)(2,1)S(1)} %bitcast.19), channel_id=1, replica_groups={{0,32,64,96,128,160,192,224,256,288,320,352,384,416,448,480},{16,48,80,..., dimensions={0} | all-to-all | bytes 1835008 | tf_op jit(solution)/shard_map/all_to_all | solution.py:19
  102.6 0.1 convert_reduce_fusion
  102.7 0.0 copy-done.2
  102.7 0.0 copy-done.3
  102.7 0.0 copy-start.1
  102.7 0.7 divide_convert_fusion
  103.5 0.1 broadcast_in_dim.32
  103.5 18.3 %all_to_all.16 = bf16[16,16,1792]{2,1,0:T(8,128)(2,1)S(1)} all-to-all(bf16[16,16,1792]{2,1,0:T(8,128)(2,1)S(1)} %broadcast_in_dim.32), channel_id=1, replica_groups={{0,32,64,96,128,160,192,224,256,288,320,352,384,416,448,480},{16,48,80,..., dimensions={0} | all-to-all | bytes 1835008 | tf_op jit(solution)/shard_map/all_to_all | solution.py:19
  121.8 1.9 %collective-permute-start.2 = (bf16[256,1792]{1,0:T(8,128)(2,1)S(1)}, bf16[256,1792]{1,0:T(8,128)(2,1)}, u32[]{:S(2)}, u32[]{:S(2)}) collective-permute-start(bf16[256,1792]{1,0:T(8,128)(2,1)S(1)} %bitcast.17), channel_id=1, source_target_pairs={{0,16},{16,0},{32,48},{48,32},{64,80},{80,64},{96,112},{112,96},{1... | collective-permute-start | bytes 2752520 | tf_op jit(solution)/shard_map/ppermute | solution.py:84
  123.7 0.0 copy-done.1
  123.8 8.3 %collective-permute-start.1 = (bf16[256,512]{1,0:T(8,128)(2,1)S(1)}, bf16[256,512]{1,0:T(8,128)(2,1)S(1)}, u32[]{:S(2)}, u32[]{:S(2)}) collective-permute-start(bf16[256,512]{1,0:T(8,128)(2,1)S(1)} %constant_dynamic-slice_fusion), channel_id=1, source_target_pairs={{0,0},{1,47},{2,78},{3,109},{4,140},{5,171},{6,202},{7,233},{8,264... | collective-permute-start | bytes 786440 | tf_op jit(solution)/shard_map/ppermute | solution.py:59
  132.1 25.5 %collective-permute-done.1 = bf16[256,512]{1,0:T(8,128)(2,1)S(1)} collective-permute-done((bf16[256,512]{1,0:T(8,128)(2,1)S(1)}, bf16[256,512]{1,0:T(8,128)(2,1)S(1)}, u32[]{:S(2)}, u32[]{:S(2)}) %collective-permute-start.1) | collective-permute-done | bytes 262176 | tf_op jit(solution)/shard_map/ppermute | solution.py:59
  157.6 0.4 convolution_convert_fusion.2
  157.9 0.4 fusion.4
  158.4 0.0 collective-permute-done.2
  158.4 2.5 %fusion.1 = bf16[256,1792]{1,0:T(8,128)(2,1)} fusion(f32[256,1792]{1,0:T(8,128)S(1)} %fusion.4, bf16[256,1792]{1,0:T(8,128)(2,1)} %collective-permute-done.2, bf16[256,512]{1,0:T(8,128)(2,1)S(1)} %convolution_convert_fusion.2), kind=kOutput, calls=%fused_computation.3 | convolution fusion | flops 236257280 | bytes 3801088 | tf_op jit(solution)/shard_map/dot_general | solution.py:92
  (5 shorter events, 0.1 us)
Async XLA Ops:
  0.6 77.2 %copy-start = (bf16[512,1792]{1,0:T(8,128)(2,1)S(1)}, bf16[512,1792]{1,0:T(8,128)(2,1)}, u32[]{:S(2)}) copy-start(bf16[512,1792]{1,0:T(8,128)(2,1)} %param.7) | copy-start | bytes 5505028
  0.6 17.8 %copy-start.4 = (s32[4]{0:T(128)S(1)}, s32[4]{0:T(128)}, u32[]{:S(2)}) copy-start(s32[4]{0:T(128)} %param.11) | copy-start | bytes 52
  3.3 43.7 %all-to-all-start = ((bf16[16,32,512]{2,1,0:T(8,128)(2,1)}), bf16[16,32,512]{2,1,0:T(8,128)(2,1)S(1)}, u32[]{:S(2)}, u32[]{:S(2)}) async-start(bf16[16,32,512]{2,1,0:T(8,128)(2,1)} %bitcast), calls=%async_computation | async-start | bytes 1048576 | tf_op jit(solution)/shard_map/all_to_all | solution.py:19
  78.5 4.4 %collective-permute-start = (bf16[256,1792]{1,0:T(8,128)(2,1)S(1)}, bf16[256,1792]{1,0:T(8,128)(2,1)S(1)}, u32[]{:S(2)}, u32[]{:S(2)}) collective-permute-start(bf16[256,1792]{1,0:T(8,128)(2,1)S(1)} %convolution_convert_fusion), channel_id=1, source_target_pairs={{0,16},{16,0},{32,48},{48,32},{64,80},{80,64},{96,112},{112,96},{1... | collective-permute-start | bytes 2752520 | tf_op jit(solution)/shard_map/ppermute | solution.py:72
  83.5 19.2 %copy-start.2 = (f32[16,1792]{1,0:T(8,128)S(1)}, f32[16,1792]{1,0:T(8,128)}, u32[]{:S(2)}) copy-start(f32[16,1792]{1,0:T(8,128)} %param.10) | copy-start | bytes 344068
  83.6 19.1 %copy-start.3 = (f32[16,1792]{1,0:T(8,128)S(1)}, f32[16,1792]{1,0:T(8,128)}, u32[]{:S(2)}) copy-start(f32[16,1792]{1,0:T(8,128)} %param.9) | copy-start | bytes 344068
  102.7 21.0 %copy-start.1 = (bf16[512,512]{1,0:T(8,128)(2,1)S(1)}, bf16[512,512]{1,0:T(8,128)(2,1)}, u32[]{:S(2)}) copy-start(bf16[512,512]{1,0:T(8,128)(2,1)} %param.8) | copy-start | bytes 1572868
  121.8 36.6 %collective-permute-start.2 = (bf16[256,1792]{1,0:T(8,128)(2,1)S(1)}, bf16[256,1792]{1,0:T(8,128)(2,1)}, u32[]{:S(2)}, u32[]{:S(2)}) collective-permute-start(bf16[256,1792]{1,0:T(8,128)(2,1)S(1)} %bitcast.17), channel_id=1, source_target_pairs={{0,16},{16,0},{32,48},{48,32},{64,80},{80,64},{96,112},{112,96},{1... | collective-permute-start | bytes 2752520 | tf_op jit(solution)/shard_map/ppermute | solution.py:84
  123.8 33.8 %collective-permute-start.1 = (bf16[256,512]{1,0:T(8,128)(2,1)S(1)}, bf16[256,512]{1,0:T(8,128)(2,1)S(1)}, u32[]{:S(2)}, u32[]{:S(2)}) collective-permute-start(bf16[256,512]{1,0:T(8,128)(2,1)S(1)} %constant_dynamic-slice_fusion), channel_id=1, source_target_pairs={{0,0},{1,47},{2,78},{3,109},{4,140},{5,171},{6,202},{7,233},{8,264... | collective-permute-start | bytes 786440 | tf_op jit(solution)/shard_map/ppermute | solution.py:59

commit v2 on v1

--- a/solution.py
+++ b/solution.py
@@ -2,6 +2,7 @@
 import jax.numpy as jnp
 from jax import lax
 from jax.sharding import PartitionSpec as P
+
 
 SLOTS = 128
 STEP = 1000
@@ -45,32 +46,43 @@
     replicas = lax.axis_size("dp")
     splits = lax.axis_size("tensor")
     chips = replicas // 2
-    replica = lax.axis_index("dp")
-    core = replica % 2
+    core = lax.axis_index("dp") % 2
+    parity = lax.axis_index("tensor") % 2
     rank = galore_basis.shape[1]
+    half = rank // 2
     owned = rank // replicas
     columns = out_grad.shape[1]
     slots = tokens.shape[0]
     same_core = [[2 * i + c for i in range(chips)] for c in range(2)]
-    partner = [(i, i ^ 1) for i in range(replicas)]
+    same_parity = [[2 * i + p for i in range(splits // 2)] for p in range(2)]
+    other_core = [(i, i ^ 1) for i in range(replicas)]
+    neighbor = [(i, i ^ 1) for i in range(splits)]
 
+    def coordinates_of(side):
+        part = lax.dynamic_slice_in_dim(galore_basis, side * half, half, 1)
+        return lax.dot_general(part, tokens, (((0,), (1,)), ((), ())), preferred_element_type=f32)
+
+    received = lax.ppermute(coordinates_of(1 - parity).astype(bf16), "tensor", neighbor)
     block_rows = galore_basis.shape[0] * splits // replicas
     half_block = lax.dynamic_slice_in_dim(galore_basis, core * block_rows, block_rows, 0)
     local_basis = lax.ppermute(half_block, ("dp", "tensor"), basis_routes(chips, splits))
-
-    partial = lax.dot_general(
-        galore_basis, tokens, (((0,), (1,)), ((), ())), preferred_element_type=f32
-    ).astype(bf16)
-    arrived = exchange(partial.reshape(splits, rank // splits, slots), "tensor")
+    pair_sum = (coordinates_of(parity) + received.astype(f32)).astype(bf16)
+    arrived = exchange(pair_sum.reshape(splits // 2, rank // splits, slots), "tensor", same_parity)
     coordinates = arrived.astype(f32).sum(axis=0)
     weighted = (coordinates * token_weights(list_lengths)[None, :]).astype(bf16)
-    weighted = lax.all_gather(weighted, "tensor", axis=0, tiled=True)
-    by_owner = weighted.reshape(chips, 2, owned, slots)
-    other = lax.dynamic_index_in_dim(by_owner, 1 - core, 1, keepdims=False).reshape(rank // 2, slots)
-    own = lax.dynamic_index_in_dim(by_owner, core, 1, keepdims=False).reshape(rank // 2, slots)
-    sent = jnp.dot(other, out_grad, preferred_element_type=f32).astype(bf16)
-    received = lax.ppermute(sent, "dp", partner)
-    kept = jnp.dot(own, out_grad, preferred_element_type=f32)
+    near = copies_to_all(weighted, "tensor", splits // 2, same_parity).reshape(half, slots)
+    far = lax.ppermute(near, "tensor", neighbor)
+
+    low = jnp.where(parity == 0, near, far).reshape(chips // 2, 2, owned, slots)
+    high = jnp.where(parity == 0, far, near).reshape(chips // 2, 2, owned, slots)
+
+    def rows_of(side):
+        parts = [lax.dynamic_index_in_dim(x, side, 1, keepdims=False) for x in (low, high)]
+        return jnp.concatenate(parts, axis=0).reshape(half, slots)
+
+    sent = jnp.dot(rows_of(1 - core), out_grad, preferred_element_type=f32).astype(bf16)
+    received = lax.ppermute(sent, "dp", other_core)
+    kept = jnp.dot(rows_of(core), out_grad, preferred_element_type=f32)
     chip_sum = (kept + received.astype(f32)).astype(bf16).reshape(chips, owned, columns)
     gradient = exchange(chip_sum, "dp", same_core).astype(f32).sum(axis=0)
 
@@ -80,16 +92,15 @@
     corrected_second = new_second / (1.0 - beta_second**STEP)
     update = (corrected_first / (jnp.sqrt(corrected_second) + epsilon)).astype(bf16)
 
-    own_rows = copies_to_all(update, "dp", chips, same_core).reshape(rank // 2, columns)
-    other_rows = lax.ppermute(own_rows, "dp", partner)
+    own_rows = copies_to_all(update, "dp", chips, same_core).reshape(half, columns)
+    other_rows = lax.ppermute(own_rows, "dp", other_core)
     place = jnp.arange(rank, dtype=jnp.int32)
-    side = place // (rank // 2)
-    within = place % (rank // 2)
-    source = (within // owned) * (2 * owned) + jnp.where(side == 0, core, 1 - core) * owned + within % owned
+    within = place % half
+    source = (within // owned) * (2 * owned) + jnp.where(place < half, core, 1 - core) * owned + within % owned
     pick = (place[:, None] == source[None, :]).astype(bf16)
     ordered = jnp.dot(local_basis, pick, preferred_element_type=f32).astype(bf16)
-    expanded = jnp.dot(ordered[:, : rank // 2], own_rows, preferred_element_type=f32)
-    expanded = expanded + jnp.dot(ordered[:, rank // 2 :], other_rows, preferred_element_type=f32)
+    expanded = jnp.dot(ordered[:, :half], own_rows, preferred_element_type=f32)
+    expanded = expanded + jnp.dot(ordered[:, half:], other_rows, preferred_element_type=f32)
     weight_step = (-expanded).astype(bf16)
     return (new_first, new_second, weight_step)
 

time: 161 us -> 164 us (1.019)
  blocking collectives: 68 us -> 60.4 us
  starting transfers between devices: 27.3 us -> 32.2 us
  waiting for transfers between devices: 56.3 us -> 60.8 us
    all_gather x1 -> x0, blocking collectives: 30.8 us -> none  [body(): weighted = lax.all_gather(weighted, 'tensor', axis=0, tiled=True)]
    all_to_all x2 -> x3, blocking collectives: 37.3 us -> 60.4 us  [exchange(): lax.all_to_all(tiles, axis, split_axis=0, concat_axis=0, tiled=True, axis...]
    ppermute x2 -> x4, waiting for transfers between devices: 2.44 us -> 15.6 us  [the longest x1 7.91 us: body(): lax.ppermute(coordinates_of(1 - parity).astype(bf16), 'tensor', neighbor)]
    all_to_all x1, waiting for transfers between devices: 28.4 us -> 19.7 us  [exchange(): lax.all_to_all(tiles, axis, split_axis=0, concat_axis=0, tiled=True, axis...]
    ppermute x2 -> x4, starting transfers between devices: 3.83 us -> 9.8 us  [the longest x1 3.95 us: body(): far = lax.ppermute(near, 'tensor', neighbor)]
    dot_general x5 -> x6, matrix products: 6.83 us -> 7.99 us  [the longest x2 3.78 us: coordinates_of(): lax.dot_general(part, tokens, (((0,), (1,)), ((), ())), preferred_element...]
  transfers between devices with their start and end apart: 4 -> 6, of which waited for: 3 -> 5; matrix products, arithmetic and copies ran while one was open for 1% -> 1% of each run, Pallas kernels for 0% -> 0%
where the time goes in v2:
time: 164 us
  waiting for transfers between devices  60.8 us (37%)
  blocking collectives  60.4 us (37%)
  starting transfers between devices  32.2 us (20%)
  matrix products  8.36 us (5%)
    all_to_all x3, blocking collectives, exchange(): lax.all_to_all(tiles, axis, split_axis=0, concat_axis=0, tiled=True, axis...  60.4 us
    ppermute x1, waiting for transfers between devices, body(): lax.ppermute(half_block, ('dp', 'tensor'), basis_routes(chips, splits))  25.5 us
    all_to_all x1, waiting for transfers between devices, exchange(): lax.all_to_all(tiles, axis, split_axis=0, concat_axis=0, tiled=True, axis...  19.7 us
    all_to_all x1, starting transfers between devices, exchange(): lax.all_to_all(tiles, axis, split_axis=0, concat_axis=0, tiled=True, axis...  14.2 us
    ppermute x1, starting transfers between devices, body(): lax.ppermute(half_block, ('dp', 'tensor'), basis_routes(chips, splits))  8.22 us
    ppermute x1, waiting for transfers between devices, body(): lax.ppermute(coordinates_of(1 - parity).astype(bf16), 'tensor', neighbor)  7.91 us
    ppermute x1, waiting for transfers between devices, body(): far = lax.ppermute(near, 'tensor', neighbor)  5.24 us
    ppermute x1, starting transfers between devices, body(): far = lax.ppermute(near, 'tensor', neighbor)  3.95 us
  transfers between devices with their start and end apart: 6, of which 5 were waited for; matrix products, arithmetic and copies ran while one was open for 1% of the time, Pallas kernels for 0%

profile of v2, /device:TPU:62, one launch (start us, length us, event | category | flops | bytes accessed | tf_op | source)
XLA Modules:
  0.0 164.0 jit_solution(2335524110468820934)
XLA Ops:
  0.6 0.0 copy-start
  0.6 0.0 copy-start.4
  0.7 1.6 convolution_convert_fusion.2
  2.3 2.0 %collective-permute-start = (bf16[256,512]{1,0:T(8,128)(2,1)S(1)}, bf16[256,512]{1,0:T(8,128)(2,1)S(1)}, u32[]{:S(2)}, u32[]{:S(2)}) collective-permute-start(bf16[256,512]{1,0:T(8,128)(2,1)S(1)} %convolution_convert_fusion.2), channel_id=1, source_target_pairs={{0,1},{1,0},{2,3},{3,2},{4,5},{5,4},{6,7},{7,6},{8,9},{9,8},{10,11... | collective-permute-start | bytes 786440 | tf_op jit(solution)/shard_map/ppermute | solution.py:65
  4.3 7.9 %collective-permute-done = bf16[256,512]{1,0:T(8,128)(2,1)S(1)} collective-permute-done((bf16[256,512]{1,0:T(8,128)(2,1)S(1)}, bf16[256,512]{1,0:T(8,128)(2,1)S(1)}, u32[]{:S(2)}, u32[]{:S(2)}) %collective-permute-start) | collective-permute-done | bytes 262176 | tf_op jit(solution)/shard_map/ppermute | solution.py:65
  12.2 2.2 %add_convert_fusion.1 = bf16[256,512]{1,0:T(8,128)(2,1)} fusion(bf16[256,512]{1,0:T(8,128)(2,1)S(1)} %collective-permute-done, bf16[512,512]{1,0:T(8,128)(2,1)} %param.6, bf16[512,512]{1,0:T(8,128)(2,1)} %param.8, s32[]{:T(128)S(6)} %select_n.91), kind=kOutput, calls=%fused_computation.11 | convolution fusion | flops 134610944 | bytes 1310724 | tf_op jit(solution)/shard_map/dot_general | solution.py:63
  14.4 14.2 %all-to-all-start = ((bf16[8,32,512]{2,1,0:T(8,128)(2,1)}), bf16[8,32,512]{2,1,0:T(8,128)(2,1)S(1)}, u32[]{:S(2)}, u32[]{:S(2)}) async-start(bf16[8,32,512]{2,1,0:T(8,128)(2,1)} %bitcast), calls=%async_computation | async-start | bytes 524288 | tf_op jit(solution)/shard_map/all_to_all | solution.py:20
  28.6 0.0 copy-done.4
  28.6 0.1 select_bitcast_fusion
  28.7 19.7 %all-to-all-done = bf16[8,32,512]{2,1,0:T(8,128)(2,1)S(1)} async-done(((bf16[8,32,512]{2,1,0:T(8,128)(2,1)}), bf16[8,32,512]{2,1,0:T(8,128)(2,1)S(1)}, u32[]{:S(2)}, u32[]{:S(2)}) %all-to-all-start) | async-done | bytes 262176 | tf_op jit(solution)/shard_map/all_to_all | solution.py:20
  48.5 23.1 %all_to_all.20 = bf16[8,32,512]{2,1,0:T(8,128)(2,1)S(1)} all-to-all(bf16[8,32,512]{2,1,0:T(8,128)(2,1)S(1)} %broadcast_in_dim.33), channel_id=1, replica_groups={{0,2,4,6,8,10,12,14},{1,3,5,7,9,11,13,15},{16,18,20,22,24,26,28,30},{17..., dimensions={0} | all-to-all | bytes 524288 | tf_op jit(solution)/shard_map/all_to_all | solution.py:20
  71.6 4.0 %collective-permute-start.1 = (bf16[256,512]{1,0:T(8,128)(2,1)S(1)}, bf16[256,512]{1,0:T(8,128)(2,1)S(1)}, u32[]{:S(2)}, u32[]{:S(2)}) collective-permute-start(bf16[256,512]{1,0:T(8,128)(2,1)S(1)} %bitcast.35), channel_id=1, source_target_pairs={{0,1},{1,0},{2,3},{3,2},{4,5},{5,4},{6,7},{7,6},{8,9},{9,8},{10,11... | collective-permute-start | bytes 786440 | tf_op jit(solution)/shard_map/ppermute | solution.py:74
  75.6 5.2 %collective-permute-done.1 = bf16[256,512]{1,0:T(8,128)(2,1)S(1)} collective-permute-done((bf16[256,512]{1,0:T(8,128)(2,1)S(1)}, bf16[256,512]{1,0:T(8,128)(2,1)S(1)}, u32[]{:S(2)}, u32[]{:S(2)}) %collective-permute-start.1) | collective-permute-done | bytes 262176 | tf_op jit(solution)/shard_map/ppermute | solution.py:74
  80.8 0.1 broadcast_select_fusion.1
  81.0 0.0 copy-done
  81.0 0.6 convolution_convert_fusion
  81.6 1.9 %collective-permute-start.2 = (bf16[256,1792]{1,0:T(8,128)(2,1)S(1)}, bf16[256,1792]{1,0:T(8,128)(2,1)S(1)}, u32[]{:S(2)}, u32[]{:S(2)}) collective-permute-start(bf16[256,1792]{1,0:T(8,128)(2,1)S(1)} %convolution_convert_fusion), channel_id=1, source_target_pairs={{0,16},{16,0},{32,48},{48,32},{64,80},{80,64},{96,112},{112,96},{1... | collective-permute-start | bytes 2752520 | tf_op jit(solution)/shard_map/ppermute | solution.py:84
  83.6 2.4 %collective-permute-done.2 = bf16[256,1792]{1,0:T(8,128)(2,1)S(1)} collective-permute-done((bf16[256,1792]{1,0:T(8,128)(2,1)S(1)}, bf16[256,1792]{1,0:T(8,128)(2,1)S(1)}, u32[]{:S(2)}, u32[]{:S(2)}) %collective-permute-start.2) | collective-permute-done | bytes 917536 | tf_op jit(solution)/shard_map/ppermute | solution.py:84
  86.0 0.6 add_convert_fusion
  86.7 0.0 copy-start.2
  86.7 0.0 copy-start.3
  86.7 19.0 %all_to_all.21 = bf16[16,16,1792]{2,1,0:T(8,128)(2,1)S(1)} all-to-all(bf16[16,16,1792]{2,1,0:T(8,128)(2,1)S(1)} %bitcast.31), channel_id=1, replica_groups={{0,32,64,96,128,160,192,224,256,288,320,352,384,416,448,480},{16,48,80,..., dimensions={0} | all-to-all | bytes 1835008 | tf_op jit(solution)/shard_map/all_to_all | solution.py:20
  105.7 0.1 convert_reduce_fusion
  105.8 0.0 copy-done.2
  105.8 0.0 copy-done.3
  105.8 0.0 copy-start.1
  105.8 0.7 divide_convert_fusion
  106.6 0.1 broadcast_in_dim.36
  106.6 18.3 %all_to_all.22 = bf16[16,16,1792]{2,1,0:T(8,128)(2,1)S(1)} all-to-all(bf16[16,16,1792]{2,1,0:T(8,128)(2,1)S(1)} %broadcast_in_dim.36), channel_id=1, replica_groups={{0,32,64,96,128,160,192,224,256,288,320,352,384,416,448,480},{16,48,80,..., dimensions={0} | all-to-all | bytes 1835008 | tf_op jit(solution)/shard_map/all_to_all | solution.py:20
  124.9 1.9 %collective-permute-start.4 = (bf16[256,1792]{1,0:T(8,128)(2,1)S(1)}, bf16[256,1792]{1,0:T(8,128)(2,1)}, u32[]{:S(2)}, u32[]{:S(2)}) collective-permute-start(bf16[256,1792]{1,0:T(8,128)(2,1)S(1)} %bitcast.29), channel_id=1, source_target_pairs={{0,16},{16,0},{32,48},{48,32},{64,80},{80,64},{96,112},{112,96},{1... | collective-permute-start | bytes 2752520 | tf_op jit(solution)/shard_map/ppermute | solution.py:96
  126.8 0.0 copy-done.1
  126.9 8.2 %collective-permute-start.3 = (bf16[256,512]{1,0:T(8,128)(2,1)S(1)}, bf16[256,512]{1,0:T(8,128)(2,1)S(1)}, u32[]{:S(2)}, u32[]{:S(2)}) collective-permute-start(bf16[256,512]{1,0:T(8,128)(2,1)S(1)} %constant_dynamic-slice_fusion), channel_id=1, source_target_pairs={{0,0},{1,47},{2,78},{3,109},{4,140},{5,171},{6,202},{7,233},{8,264... | collective-permute-start | bytes 786440 | tf_op jit(solution)/shard_map/ppermute | solution.py:68
  135.1 25.5 %collective-permute-done.3 = bf16[256,512]{1,0:T(8,128)(2,1)S(1)} collective-permute-done((bf16[256,512]{1,0:T(8,128)(2,1)S(1)}, bf16[256,512]{1,0:T(8,128)(2,1)S(1)}, u32[]{:S(2)}, u32[]{:S(2)}) %collective-permute-start.3) | collective-permute-done | bytes 262176 | tf_op jit(solution)/shard_map/ppermute | solution.py:68
  160.6 0.4 convolution_convert_fusion.1
  161.0 0.4 fusion.9
  161.4 0.0 collective-permute-done.4
  161.5 2.5 %fusion.1 = bf16[256,1792]{1,0:T(8,128)(2,1)} fusion(f32[256,1792]{1,0:T(8,128)S(1)} %fusion.9, bf16[256,1792]{1,0:T(8,128)(2,1)} %collective-permute-done.4, bf16[256,512]{1,0:T(8,128)(2,1)S(1)} %convolution_convert_fusion.1), kind=kOutput, calls=%fused_computation.3 | convolution fusion | flops 236257280 | bytes 3801088 | tf_op jit(solution)/shard_map/dot_general | solution.py:103
  (9 shorter events, 0.2 us)
Async XLA Ops:
  0.6 80.4 %copy-start = (bf16[512,1792]{1,0:T(8,128)(2,1)S(1)}, bf16[512,1792]{1,0:T(8,128)(2,1)}, u32[]{:S(2)}) copy-start(bf16[512,1792]{1,0:T(8,128)(2,1)} %param.7) | copy-start | bytes 5505028
  0.6 27.9 %copy-start.4 = (s32[4]{0:T(128)S(1)}, s32[4]{0:T(128)}, u32[]{:S(2)}) copy-start(s32[4]{0:T(128)} %param.11) | copy-start | bytes 52
  2.3 9.9 %collective-permute-start = (bf16[256,512]{1,0:T(8,128)(2,1)S(1)}, bf16[256,512]{1,0:T(8,128)(2,1)S(1)}, u32[]{:S(2)}, u32[]{:S(2)}) collective-permute-start(bf16[256,512]{1,0:T(8,128)(2,1)S(1)} %convolution_convert_fusion.2), channel_id=1, source_target_pairs={{0,1},{1,0},{2,3},{3,2},{4,5},{5,4},{6,7},{7,6},{8,9},{9,8},{10,11... | collective-permute-start | bytes 786440 | tf_op jit(solution)/shard_map/ppermute | solution.py:65
  14.4 34.0 %all-to-all-start = ((bf16[8,32,512]{2,1,0:T(8,128)(2,1)}), bf16[8,32,512]{2,1,0:T(8,128)(2,1)S(1)}, u32[]{:S(2)}, u32[]{:S(2)}) async-start(bf16[8,32,512]{2,1,0:T(8,128)(2,1)} %bitcast), calls=%async_computation | async-start | bytes 524288 | tf_op jit(solution)/shard_map/all_to_all | solution.py:20
  71.6 9.2 %collective-permute-start.1 = (bf16[256,512]{1,0:T(8,128)(2,1)S(1)}, bf16[256,512]{1,0:T(8,128)(2,1)S(1)}, u32[]{:S(2)}, u32[]{:S(2)}) collective-permute-start(bf16[256,512]{1,0:T(8,128)(2,1)S(1)} %bitcast.35), channel_id=1, source_target_pairs={{0,1},{1,0},{2,3},{3,2},{4,5},{5,4},{6,7},{7,6},{8,9},{9,8},{10,11... | collective-permute-start | bytes 786440 | tf_op jit(solution)/shard_map/ppermute | solution.py:74
  81.6 4.4 %collective-permute-start.2 = (bf16[256,1792]{1,0:T(8,128)(2,1)S(1)}, bf16[256,1792]{1,0:T(8,128)(2,1)S(1)}, u32[]{:S(2)}, u32[]{:S(2)}) collective-permute-start(bf16[256,1792]{1,0:T(8,128)(2,1)S(1)} %convolution_convert_fusion), channel_id=1, source_target_pairs={{0,16},{16,0},{32,48},{48,32},{64,80},{80,64},{96,112},{112,96},{1... | collective-permute-start | bytes 2752520 | tf_op jit(solution)/shard_map/ppermute | solution.py:84
  86.7 19.1 %copy-start.2 = (f32[16,1792]{1,0:T(8,128)S(1)}, f32[16,1792]{1,0:T(8,128)}, u32[]{:S(2)}) copy-start(f32[16,1792]{1,0:T(8,128)} %param.10) | copy-start | bytes 344068
  86.7 19.1 %copy-start.3 = (f32[16,1792]{1,0:T(8,128)S(1)}, f32[16,1792]{1,0:T(8,128)}, u32[]{:S(2)}) copy-start(f32[16,1792]{1,0:T(8,128)} %param.9) | copy-start | bytes 344068
  105.8 21.0 %copy-start.1 = (bf16[512,512]{1,0:T(8,128)(2,1)S(1)}, bf16[512,512]{1,0:T(8,128)(2,1)}, u32[]{:S(2)}) copy-start(bf16[512,512]{1,0:T(8,128)(2,1)} %param.8) | copy-start | bytes 1572868
  124.9 36.6 %collective-permute-start.4 = (bf16[256,1792]{1,0:T(8,128)(2,1)S(1)}, bf16[256,1792]{1,0:T(8,128)(2,1)}, u32[]{:S(2)}, u32[]{:S(2)}) collective-permute-start(bf16[256,1792]{1,0:T(8,128)(2,1)S(1)} %bitcast.29), channel_id=1, source_target_pairs={{0,16},{16,0},{32,48},{48,32},{64,80},{80,64},{96,112},{112,96},{1... | collective-permute-start | bytes 2752520 | tf_op jit(solution)/shard_map/ppermute | solution.py:96
  126.9 33.8 %collective-permute-start.3 = (bf16[256,512]{1,0:T(8,128)(2,1)S(1)}, bf16[256,512]{1,0:T(8,128)(2,1)S(1)}, u32[]{:S(2)}, u32[]{:S(2)}) collective-permute-start(bf16[256,512]{1,0:T(8,128)(2,1)S(1)} %constant_dynamic-slice_fusion), channel_id=1, source_target_pairs={{0,0},{1,47},{2,78},{3,109},{4,140},{5,171},{6,202},{7,233},{8,264... | collective-permute-start | bytes 786440 | tf_op jit(solution)/shard_map/ppermute | solution.py:68

commit v3 on v2

--- a/solution.py
+++ b/solution.py
@@ -66,7 +66,8 @@
     block_rows = galore_basis.shape[0] * splits // replicas
     half_block = lax.dynamic_slice_in_dim(galore_basis, core * block_rows, block_rows, 0)
     local_basis = lax.ppermute(half_block, ("dp", "tensor"), basis_routes(chips, splits))
-    pair_sum = (coordinates_of(parity) + received.astype(f32)).astype(bf16)
+    kept = lax.optimization_barrier(coordinates_of(parity))
+    pair_sum = (kept + received.astype(f32)).astype(bf16)
     arrived = exchange(pair_sum.reshape(splits // 2, rank // splits, slots), "tensor", same_parity)
     coordinates = arrived.astype(f32).sum(axis=0)
     weighted = (coordinates * token_weights(list_lengths)[None, :]).astype(bf16)
@@ -82,7 +83,7 @@
 
     sent = jnp.dot(rows_of(1 - core), out_grad, preferred_element_type=f32).astype(bf16)
     received = lax.ppermute(sent, "dp", other_core)
-    kept = jnp.dot(rows_of(core), out_grad, preferred_element_type=f32)
+    kept = lax.optimization_barrier(jnp.dot(rows_of(core), out_grad, preferred_element_type=f32))
     chip_sum = (kept + received.astype(f32)).astype(bf16).reshape(chips, owned, columns)
     gradient = exchange(chip_sum, "dp", same_core).astype(f32).sum(axis=0)
 

time: 164 us -> 163 us (level)
  waiting for transfers between devices: 60.8 us -> 58.7 us
  transfers between devices with their start and end apart: 6 -> 6, of which waited for: 5 -> 5; matrix products, arithmetic and copies ran while one was open for 1% -> 2% of each run, Pallas kernels for 0% -> 0%
where the time goes in v3:
time: 163 us; the launch traced here: 162 us
  blocking collectives  60.4 us (37%)
  waiting for transfers between devices  58.7 us (36%)
  starting transfers between devices  32.2 us (20%)
  matrix products  7.66 us (5%)
  other arithmetic  2.07 us (1%)
    all_to_all x3, blocking collectives, exchange(): lax.all_to_all(tiles, axis, split_axis=0, concat_axis=0, tiled=True, axis...  60.4 us
    ppermute x1, waiting for transfers between devices, body(): lax.ppermute(half_block, ('dp', 'tensor'), basis_routes(chips, splits))  25.6 us
    all_to_all x1, waiting for transfers between devices, exchange(): lax.all_to_all(tiles, axis, split_axis=0, concat_axis=0, tiled=True, axis...  19.7 us
    all_to_all x1, starting transfers between devices, exchange(): lax.all_to_all(tiles, axis, split_axis=0, concat_axis=0, tiled=True, axis...  14.2 us
    ppermute x1, starting transfers between devices, body(): lax.ppermute(half_block, ('dp', 'tensor'), basis_routes(chips, splits))  8.21 us
    ppermute x1, waiting for transfers between devices, body(): lax.ppermute(coordinates_of(1 - parity).astype(bf16), 'tensor', neighbor)  6.42 us
    ppermute x1, waiting for transfers between devices, body(): far = lax.ppermute(near, 'tensor', neighbor)  5.24 us
    ppermute x1, starting transfers between devices, body(): far = lax.ppermute(near, 'tensor', neighbor)  3.95 us
  transfers between devices with their start and end apart: 6, of which 5 were waited for; matrix products, arithmetic and copies ran while one was open for 2% of the time, Pallas kernels for 0%

profile of v3, /device:TPU:62, one launch (start us, length us, event | category | flops | bytes accessed | tf_op | source)
XLA Modules:
  0.0 162.1 jit_solution(7354373547286293092)
XLA Ops:
  0.6 0.0 copy-start
  0.7 0.0 copy-start.4
  0.7 1.6 convolution_convert_fusion.2
  2.3 2.0 %collective-permute-start = (bf16[256,512]{1,0:T(8,128)(2,1)S(1)}, bf16[256,512]{1,0:T(8,128)(2,1)S(1)}, u32[]{:S(2)}, u32[]{:S(2)}) collective-permute-start(bf16[256,512]{1,0:T(8,128)(2,1)S(1)} %convolution_convert_fusion.2), channel_id=1, source_target_pairs={{0,1},{1,0},{2,3},{3,2},{4,5},{5,4},{6,7},{7,6},{8,9},{9,8},{10,11... | collective-permute-start | bytes 786440 | tf_op jit(solution)/shard_map/ppermute | solution.py:65
  4.3 1.5 fusion.4
  5.8 6.4 %collective-permute-done = bf16[256,512]{1,0:T(8,128)(2,1)S(1)} collective-permute-done((bf16[256,512]{1,0:T(8,128)(2,1)S(1)}, bf16[256,512]{1,0:T(8,128)(2,1)S(1)}, u32[]{:S(2)}, u32[]{:S(2)}) %collective-permute-start) | collective-permute-done | bytes 262176 | tf_op jit(solution)/shard_map/ppermute | solution.py:65
  12.2 0.8 add_convert_fusion.1
  13.0 14.2 %all-to-all-start = ((bf16[8,32,512]{2,1,0:T(8,128)(2,1)}), bf16[8,32,512]{2,1,0:T(8,128)(2,1)S(1)}, u32[]{:S(2)}, u32[]{:S(2)}) async-start(bf16[8,32,512]{2,1,0:T(8,128)(2,1)} %bitcast), calls=%async_computation | async-start | bytes 524288 | tf_op jit(solution)/shard_map/all_to_all | solution.py:20
  27.2 0.0 copy-done.4
  27.2 0.1 select_bitcast_fusion
  27.3 19.7 %all-to-all-done = bf16[8,32,512]{2,1,0:T(8,128)(2,1)S(1)} async-done(((bf16[8,32,512]{2,1,0:T(8,128)(2,1)}), bf16[8,32,512]{2,1,0:T(8,128)(2,1)S(1)}, u32[]{:S(2)}, u32[]{:S(2)}) %all-to-all-start) | async-done | bytes 262176 | tf_op jit(solution)/shard_map/all_to_all | solution.py:20
  47.1 23.1 %all_to_all.20 = bf16[8,32,512]{2,1,0:T(8,128)(2,1)S(1)} all-to-all(bf16[8,32,512]{2,1,0:T(8,128)(2,1)S(1)} %broadcast_in_dim.33), channel_id=1, replica_groups={{0,2,4,6,8,10,12,14},{1,3,5,7,9,11,13,15},{16,18,20,22,24,26,28,30},{17..., dimensions={0} | all-to-all | bytes 524288 | tf_op jit(solution)/shard_map/all_to_all | solution.py:20
  70.2 3.9 %collective-permute-start.1 = (bf16[256,512]{1,0:T(8,128)(2,1)S(1)}, bf16[256,512]{1,0:T(8,128)(2,1)S(1)}, u32[]{:S(2)}, u32[]{:S(2)}) collective-permute-start(bf16[256,512]{1,0:T(8,128)(2,1)S(1)} %bitcast.35), channel_id=1, source_target_pairs={{0,1},{1,0},{2,3},{3,2},{4,5},{5,4},{6,7},{7,6},{8,9},{9,8},{10,11... | collective-permute-start | bytes 786440 | tf_op jit(solution)/shard_map/ppermute | solution.py:75
  74.2 5.2 %collective-permute-done.1 = bf16[256,512]{1,0:T(8,128)(2,1)S(1)} collective-permute-done((bf16[256,512]{1,0:T(8,128)(2,1)S(1)}, bf16[256,512]{1,0:T(8,128)(2,1)S(1)}, u32[]{:S(2)}, u32[]{:S(2)}) %collective-permute-start.1) | collective-permute-done | bytes 262176 | tf_op jit(solution)/shard_map/ppermute | solution.py:75
  79.4 0.1 broadcast_select_fusion.1
  79.6 0.0 copy-done
  79.6 0.6 convolution_convert_fusion
  80.2 1.9 %collective-permute-start.2 = (bf16[256,1792]{1,0:T(8,128)(2,1)S(1)}, bf16[256,1792]{1,0:T(8,128)(2,1)S(1)}, u32[]{:S(2)}, u32[]{:S(2)}) collective-permute-start(bf16[256,1792]{1,0:T(8,128)(2,1)S(1)} %convolution_convert_fusion), channel_id=1, source_target_pairs={{0,16},{16,0},{32,48},{48,32},{64,80},{80,64},{96,112},{112,96},{1... | collective-permute-start | bytes 2752520 | tf_op jit(solution)/shard_map/ppermute | solution.py:85
  82.2 0.6 fusion.22
  82.9 1.8 %collective-permute-done.2 = bf16[256,1792]{1,0:T(8,128)(2,1)S(1)} collective-permute-done((bf16[256,1792]{1,0:T(8,128)(2,1)S(1)}, bf16[256,1792]{1,0:T(8,128)(2,1)S(1)}, u32[]{:S(2)}, u32[]{:S(2)}) %collective-permute-start.2) | collective-permute-done | bytes 917536 | tf_op jit(solution)/shard_map/ppermute | solution.py:85
  84.6 0.2 add_convert_fusion
  84.8 0.0 copy-start.2
  84.8 0.0 copy-start.3
  84.8 19.0 %all_to_all.21 = bf16[16,16,1792]{2,1,0:T(8,128)(2,1)S(1)} all-to-all(bf16[16,16,1792]{2,1,0:T(8,128)(2,1)S(1)} %bitcast.29), channel_id=1, replica_groups={{0,32,64,96,128,160,192,224,256,288,320,352,384,416,448,480},{16,48,80,..., dimensions={0} | all-to-all | bytes 1835008 | tf_op jit(solution)/shard_map/all_to_all | solution.py:20
  103.8 0.1 convert_reduce_fusion
  103.9 0.0 copy-done.2
  103.9 0.0 copy-done.3
  103.9 0.0 copy-start.1
  104.0 0.8 divide_convert_fusion
  104.7 0.1 broadcast_in_dim.36
  104.8 18.3 %all_to_all.22 = bf16[16,16,1792]{2,1,0:T(8,128)(2,1)S(1)} all-to-all(bf16[16,16,1792]{2,1,0:T(8,128)(2,1)S(1)} %broadcast_in_dim.36), channel_id=1, replica_groups={{0,32,64,96,128,160,192,224,256,288,320,352,384,416,448,480},{16,48,80,..., dimensions={0} | all-to-all | bytes 1835008 | tf_op jit(solution)/shard_map/all_to_all | solution.py:20
  123.0 1.9 %collective-permute-start.4 = (bf16[256,1792]{1,0:T(8,128)(2,1)S(1)}, bf16[256,1792]{1,0:T(8,128)(2,1)}, u32[]{:S(2)}, u32[]{:S(2)}) collective-permute-start(bf16[256,1792]{1,0:T(8,128)(2,1)S(1)} %bitcast.30), channel_id=1, source_target_pairs={{0,16},{16,0},{32,48},{48,32},{64,80},{80,64},{96,112},{112,96},{1... | collective-permute-start | bytes 2752520 | tf_op jit(solution)/shard_map/ppermute | solution.py:97
  125.0 0.0 copy-done.1
  125.0 8.2 %collective-permute-start.3 = (bf16[256,512]{1,0:T(8,128)(2,1)S(1)}, bf16[256,512]{1,0:T(8,128)(2,1)S(1)}, u32[]{:S(2)}, u32[]{:S(2)}) collective-permute-start(bf16[256,512]{1,0:T(8,128)(2,1)S(1)} %constant_dynamic-slice_fusion), channel_id=1, source_target_pairs={{0,0},{1,47},{2,78},{3,109},{4,140},{5,171},{6,202},{7,233},{8,264... | collective-permute-start | bytes 786440 | tf_op jit(solution)/shard_map/ppermute | solution.py:68
  133.2 25.6 %collective-permute-done.3 = bf16[256,512]{1,0:T(8,128)(2,1)S(1)} collective-permute-done((bf16[256,512]{1,0:T(8,128)(2,1)S(1)}, bf16[256,512]{1,0:T(8,128)(2,1)S(1)}, u32[]{:S(2)}, u32[]{:S(2)}) %collective-permute-start.3) | collective-permute-done | bytes 262176 | tf_op jit(solution)/shard_map/ppermute | solution.py:68
  158.8 0.4 convolution_convert_fusion.1
  159.2 0.4 fusion.7
  159.6 0.0 collective-permute-done.4
  159.6 2.5 %fusion.1 = bf16[256,1792]{1,0:T(8,128)(2,1)} fusion(f32[256,1792]{1,0:T(8,128)S(1)} %fusion.7, bf16[256,1792]{1,0:T(8,128)(2,1)} %collective-permute-done.4, bf16[256,512]{1,0:T(8,128)(2,1)S(1)} %convolution_convert_fusion.1), kind=kOutput, calls=%fused_computation.3 | convolution fusion | flops 236257280 | bytes 3801088 | tf_op jit(solution)/shard_map/dot_general | solution.py:104
  (9 shorter events, 0.2 us)
Async XLA Ops:
  0.6 79.0 %copy-start = (bf16[512,1792]{1,0:T(8,128)(2,1)S(1)}, bf16[512,1792]{1,0:T(8,128)(2,1)}, u32[]{:S(2)}) copy-start(bf16[512,1792]{1,0:T(8,128)(2,1)} %param.7) | copy-start | bytes 5505028
  0.7 26.5 %copy-start.4 = (s32[4]{0:T(128)S(1)}, s32[4]{0:T(128)}, u32[]{:S(2)}) copy-start(s32[4]{0:T(128)} %param.11) | copy-start | bytes 52
  2.3 9.9 %collective-permute-start = (bf16[256,512]{1,0:T(8,128)(2,1)S(1)}, bf16[256,512]{1,0:T(8,128)(2,1)S(1)}, u32[]{:S(2)}, u32[]{:S(2)}) collective-permute-start(bf16[256,512]{1,0:T(8,128)(2,1)S(1)} %convolution_convert_fusion.2), channel_id=1, source_target_pairs={{0,1},{1,0},{2,3},{3,2},{4,5},{5,4},{6,7},{7,6},{8,9},{9,8},{10,11... | collective-permute-start | bytes 786440 | tf_op jit(solution)/shard_map/ppermute | solution.py:65
  13.0 34.0 %all-to-all-start = ((bf16[8,32,512]{2,1,0:T(8,128)(2,1)}), bf16[8,32,512]{2,1,0:T(8,128)(2,1)S(1)}, u32[]{:S(2)}, u32[]{:S(2)}) async-start(bf16[8,32,512]{2,1,0:T(8,128)(2,1)} %bitcast), calls=%async_computation | async-start | bytes 524288 | tf_op jit(solution)/shard_map/all_to_all | solution.py:20
  70.2 9.2 %collective-permute-start.1 = (bf16[256,512]{1,0:T(8,128)(2,1)S(1)}, bf16[256,512]{1,0:T(8,128)(2,1)S(1)}, u32[]{:S(2)}, u32[]{:S(2)}) collective-permute-start(bf16[256,512]{1,0:T(8,128)(2,1)S(1)} %bitcast.35), channel_id=1, source_target_pairs={{0,1},{1,0},{2,3},{3,2},{4,5},{5,4},{6,7},{7,6},{8,9},{9,8},{10,11... | collective-permute-start | bytes 786440 | tf_op jit(solution)/shard_map/ppermute | solution.py:75
  80.2 4.4 %collective-permute-start.2 = (bf16[256,1792]{1,0:T(8,128)(2,1)S(1)}, bf16[256,1792]{1,0:T(8,128)(2,1)S(1)}, u32[]{:S(2)}, u32[]{:S(2)}) collective-permute-start(bf16[256,1792]{1,0:T(8,128)(2,1)S(1)} %convolution_convert_fusion), channel_id=1, source_target_pairs={{0,16},{16,0},{32,48},{48,32},{64,80},{80,64},{96,112},{112,96},{1... | collective-permute-start | bytes 2752520 | tf_op jit(solution)/shard_map/ppermute | solution.py:85
  84.8 19.1 %copy-start.2 = (f32[16,1792]{1,0:T(8,128)S(1)}, f32[16,1792]{1,0:T(8,128)}, u32[]{:S(2)}) copy-start(f32[16,1792]{1,0:T(8,128)} %param.10) | copy-start | bytes 344068
  84.8 19.1 %copy-start.3 = (f32[16,1792]{1,0:T(8,128)S(1)}, f32[16,1792]{1,0:T(8,128)}, u32[]{:S(2)}) copy-start(f32[16,1792]{1,0:T(8,128)} %param.9) | copy-start | bytes 344068
  103.9 21.0 %copy-start.1 = (bf16[512,512]{1,0:T(8,128)(2,1)S(1)}, bf16[512,512]{1,0:T(8,128)(2,1)}, u32[]{:S(2)}) copy-start(bf16[512,512]{1,0:T(8,128)(2,1)} %param.8) | copy-start | bytes 1572868
  123.0 36.6 %collective-permute-start.4 = (bf16[256,1792]{1,0:T(8,128)(2,1)S(1)}, bf16[256,1792]{1,0:T(8,128)(2,1)}, u32[]{:S(2)}, u32[]{:S(2)}) collective-permute-start(bf16[256,1792]{1,0:T(8,128)(2,1)S(1)} %bitcast.30), channel_id=1, source_target_pairs={{0,16},{16,0},{32,48},{48,32},{64,80},{80,64},{96,112},{112,96},{1... | collective-permute-start | bytes 2752520 | tf_op jit(solution)/shard_map/ppermute | solution.py:97
  125.0 33.8 %collective-permute-start.3 = (bf16[256,512]{1,0:T(8,128)(2,1)S(1)}, bf16[256,512]{1,0:T(8,128)(2,1)S(1)}, u32[]{:S(2)}, u32[]{:S(2)}) collective-permute-start(bf16[256,512]{1,0:T(8,128)(2,1)S(1)} %constant_dynamic-slice_fusion), channel_id=1, source_target_pairs={{0,0},{1,47},{2,78},{3,109},{4,140},{5,171},{6,202},{7,233},{8,264... | collective-permute-start | bytes 786440 | tf_op jit(solution)/shard_map/ppermute | solution.py:68

commit v4 on v3

--- a/solution.py
+++ b/solution.py
@@ -35,7 +35,7 @@
 
 def basis_routes(chips, splits):
     return [
-        ((2 * k + b) * splits + s, (2 * s + b) * splits + (k - s) % splits)
+        ((2 * k + b) * splits + s, (2 * s + b) * splits + (k - 3 * s) % splits)
         for k in range(chips)
         for b in range(2)
         for s in range(splits)
@@ -69,22 +69,21 @@
     kept = lax.optimization_barrier(coordinates_of(parity))
     pair_sum = (kept + received.astype(f32)).astype(bf16)
     arrived = exchange(pair_sum.reshape(splits // 2, rank // splits, slots), "tensor", same_parity)
+    partner_grad = lax.ppermute(out_grad, "dp", other_core)
+    both_grads = lax.optimization_barrier(jnp.concatenate([out_grad, partner_grad], axis=0))
     coordinates = arrived.astype(f32).sum(axis=0)
     weighted = (coordinates * token_weights(list_lengths)[None, :]).astype(bf16)
-    near = copies_to_all(weighted, "tensor", splits // 2, same_parity).reshape(half, slots)
+    by_core = weighted.reshape(2, owned, slots)
+    own = lax.dynamic_index_in_dim(by_core, core, 0, keepdims=False)
+    traded = lax.ppermute(lax.dynamic_index_in_dim(by_core, 1 - core, 0, keepdims=False), "dp", other_core)
+    both = jnp.concatenate([own, traded], axis=1)
+    near = copies_to_all(both, "tensor", splits // 2, same_parity).reshape(half // 2, 2 * slots)
     far = lax.ppermute(near, "tensor", neighbor)
-
-    low = jnp.where(parity == 0, near, far).reshape(chips // 2, 2, owned, slots)
-    high = jnp.where(parity == 0, far, near).reshape(chips // 2, 2, owned, slots)
-
-    def rows_of(side):
-        parts = [lax.dynamic_index_in_dim(x, side, 1, keepdims=False) for x in (low, high)]
-        return jnp.concatenate(parts, axis=0).reshape(half, slots)
-
-    sent = jnp.dot(rows_of(1 - core), out_grad, preferred_element_type=f32).astype(bf16)
-    received = lax.ppermute(sent, "dp", other_core)
-    kept = lax.optimization_barrier(jnp.dot(rows_of(core), out_grad, preferred_element_type=f32))
-    chip_sum = (kept + received.astype(f32)).astype(bf16).reshape(chips, owned, columns)
+    low = jnp.where(parity == 0, near, far)
+    high = jnp.where(parity == 0, far, near)
+    rows = jnp.concatenate([low, high], axis=0)
+    chip_sum = jnp.dot(rows, both_grads, preferred_element_type=f32).astype(bf16)
+    chip_sum = chip_sum.reshape(chips, owned, columns)
     gradient = exchange(chip_sum, "dp", same_core).astype(f32).sum(axis=0)
 
     new_first = beta_first * first_moment + (1.0 - beta_first) * gradient

time: 163 us -> 161 us (0.988)
  the two profiles are of different devices: /device:TPU:62 before, /device:TPU:26 now
where the time goes in v4:
time: 161 us; the launch traced here: 160 us
  waiting for transfers between devices  78.3 us (49%)
  blocking collectives  35.9 us (22%)
  starting transfers between devices  33.3 us (21%)
  matrix products  6.17 us (4%)
  other arithmetic  3.59 us (2%)
  local copies, waits for them, and re-layouts  1.87 us (1%)
    all_to_all x2, waiting for transfers between devices, exchange(): lax.all_to_all(tiles, axis, split_axis=0, concat_axis=0, tiled=True, axis...  39.7 us
    all_to_all x2, blocking collectives, exchange(): lax.all_to_all(tiles, axis, split_axis=0, concat_axis=0, tiled=True, axis...  35.9 us
    ppermute x1, waiting for transfers between devices, body(): lax.ppermute(half_block, ('dp', 'tensor'), basis_routes(chips, splits))  26.2 us
    all_to_all x2, starting transfers between devices, exchange(): lax.all_to_all(tiles, axis, split_axis=0, concat_axis=0, tiled=True, axis...  18.3 us
    ppermute x1, waiting for transfers between devices, body(): far = lax.ppermute(near, 'tensor', neighbor)  6.36 us
    ppermute x1, waiting for transfers between devices, body(): lax.ppermute(coordinates_of(1 - parity).astype(bf16), 'tensor', neighbor)  4.88 us
    ppermute x1, starting transfers between devices, body(): lax.ppermute(coordinates_of(1 - parity).astype(bf16), 'tensor', neighbor)  3.83 us
    ppermute x1, starting transfers between devices, body(): lax.ppermute(half_block, ('dp', 'tensor'), basis_routes(chips, splits))  3.41 us
  transfers between devices with their start and end apart: 8, of which 6 were waited for; matrix products, arithmetic and copies ran while one was open for 3% of the time, Pallas kernels for 0%

profile of v4, /device:TPU:26, one launch (start us, length us, event | category | flops | bytes accessed | tf_op | source)
XLA Modules:
  0.0 160.0 jit_solution(16152797813305862993)
XLA Ops:
  0.6 0.0 copy-start
  0.7 1.0 copy-done
  1.7 0.0 copy-start.1
  1.7 0.0 copy-start.4
  1.7 1.5 convolution_convert_fusion.2
  3.2 3.8 %collective-permute-start = (bf16[256,512]{1,0:T(8,128)(2,1)S(1)}, bf16[256,512]{1,0:T(8,128)(2,1)S(1)}, u32[]{:S(2)}, u32[]{:S(2)}) collective-permute-start(bf16[256,512]{1,0:T(8,128)(2,1)S(1)} %convolution_convert_fusion.2), channel_id=1, source_target_pairs={{0,1},{1,0},{2,3},{3,2},{4,5},{5,4},{6,7},{7,6},{8,9},{9,8},{10,11... | collective-permute-start | bytes 786440 | tf_op jit(solution)/shard_map/ppermute | solution.py:65
  7.1 1.4 fusion.7
  8.5 4.9 %collective-permute-done = bf16[256,512]{1,0:T(8,128)(2,1)S(1)} collective-permute-done((bf16[256,512]{1,0:T(8,128)(2,1)S(1)}, bf16[256,512]{1,0:T(8,128)(2,1)S(1)}, u32[]{:S(2)}, u32[]{:S(2)}) %collective-permute-start) | collective-permute-done | bytes 262176 | tf_op jit(solution)/shard_map/ppermute | solution.py:65
  13.3 0.8 add_convert_fusion
  14.1 14.9 %all-to-all-start = ((bf16[8,32,512]{2,1,0:T(8,128)(2,1)}), bf16[8,32,512]{2,1,0:T(8,128)(2,1)S(1)}, u32[]{:S(2)}, u32[]{:S(2)}) async-start(bf16[8,32,512]{2,1,0:T(8,128)(2,1)} %bitcast), calls=%async_computation | async-start | bytes 524288 | tf_op jit(solution)/shard_map/all_to_all | solution.py:20
  29.0 0.0 copy-done.1
  29.0 1.9 %collective-permute-start.3 = (bf16[512,1792]{1,0:T(8,128)(2,1)S(1)}, bf16[512,1792]{1,0:T(8,128)(2,1)}, u32[]{:S(2)}, u32[]{:S(2)}) collective-permute-start(bf16[512,1792]{1,0:T(8,128)(2,1)S(1)} %copy-done.1), channel_id=1, source_target_pairs={{0,16},{16,0},{32,48},{48,32},{64,80},{80,64},{96,112},{112,96},{1... | collective-permute-start | bytes 5505032 | tf_op jit(solution)/shard_map/ppermute | solution.py:72
  31.0 0.0 copy-done.4
  31.0 0.1 select_bitcast_fusion
  31.1 18.4 %all-to-all-done = bf16[8,32,512]{2,1,0:T(8,128)(2,1)S(1)} async-done(((bf16[8,32,512]{2,1,0:T(8,128)(2,1)}), bf16[8,32,512]{2,1,0:T(8,128)(2,1)S(1)}, u32[]{:S(2)}, u32[]{:S(2)}) %all-to-all-start) | async-done | bytes 262176 | tf_op jit(solution)/shard_map/all_to_all | solution.py:20
  49.6 1.9 %collective-permute-start.1 = (bf16[16,512]{1,0:T(8,128)(2,1)S(1)}, bf16[16,512]{1,0:T(8,128)(2,1)S(1)}, u32[]{:S(2)}, u32[]{:S(2)}) collective-permute-start(bf16[16,512]{1,0:T(8,128)(2,1)S(1)} %get-tuple-element.9), channel_id=1, source_target_pairs={{0,16},{16,0},{32,48},{48,32},{64,80},{80,64},{96,112},{112,96},{1... | collective-permute-start | bytes 49160 | tf_op jit(solution)/shard_map/ppermute | solution.py:78
  51.5 1.1 collective-permute-done.1
  52.7 0.7 broadcast_in_dim.33
  53.4 3.4 %all-to-all-start.1 = ((bf16[8,16,1024]{2,1,0:T(8,128)(2,1)}), bf16[8,16,1024]{2,1,0:T(8,128)(2,1)S(1)}, u32[]{:S(2)}, u32[]{:S(2)}) async-start(bf16[8,16,1024]{2,1,0:T(8,128)(2,1)} %broadcast_in_dim.33), calls=%async_computation.1 | async-start | bytes 524288 | tf_op jit(solution)/shard_map/all_to_all | solution.py:20
  56.8 21.3 %all-to-all-done.1 = bf16[8,16,1024]{2,1,0:T(8,128)(2,1)S(1)} async-done(((bf16[8,16,1024]{2,1,0:T(8,128)(2,1)}), bf16[8,16,1024]{2,1,0:T(8,128)(2,1)S(1)}, u32[]{:S(2)}, u32[]{:S(2)}) %all-to-all-start.1) | async-done | bytes 262176 | tf_op jit(solution)/shard_map/all_to_all | solution.py:20
  78.1 2.0 %collective-permute-start.2 = (bf16[128,1024]{1,0:T(8,128)(2,1)S(1)}, bf16[128,1024]{1,0:T(8,128)(2,1)S(1)}, u32[]{:S(2)}, u32[]{:S(2)}) collective-permute-start(bf16[128,1024]{1,0:T(8,128)(2,1)S(1)} %bitcast.21), channel_id=1, source_target_pairs={{0,1},{1,0},{2,3},{3,2},{4,5},{5,4},{6,7},{7,6},{8,9},{9,8},{10,11... | collective-permute-start | bytes 786440 | tf_op jit(solution)/shard_map/ppermute | solution.py:81
  80.1 0.0 collective-permute-done.3
  80.1 1.7 %pad_maximum_fusion = bf16[1024,1792]{1,0:T(8,128)(2,1)S(1)} fusion(bf16[512,1792]{1,0:T(8,128)(2,1)} %collective-permute-done.3, bf16[512,1792]{1,0:T(8,128)(2,1)S(1)} %copy-done.1), kind=kLoop, calls=%fused_computation | loop fusion | flops 7340032 | bytes 7340032 | tf_op jit(solution)/shard_map/concatenate | solution.py:73
  81.8 6.4 %collective-permute-done.2 = bf16[128,1024]{1,0:T(8,128)(2,1)S(1)} collective-permute-done((bf16[128,1024]{1,0:T(8,128)(2,1)S(1)}, bf16[128,1024]{1,0:T(8,128)(2,1)S(1)}, u32[]{:S(2)}, u32[]{:S(2)}) %collective-permute-start.2) | collective-permute-done | bytes 262176 | tf_op jit(solution)/shard_map/ppermute | solution.py:81
  88.2 0.1 broadcast_select_fusion.1
  88.3 1.1 convolution_convert_fusion
  89.4 0.0 copy-start.2
  89.4 0.0 copy-start.3
  89.4 19.0 %all_to_all.20 = bf16[16,16,1792]{2,1,0:T(8,128)(2,1)S(1)} all-to-all(bf16[16,16,1792]{2,1,0:T(8,128)(2,1)S(1)} %bitcast.22), channel_id=1, replica_groups={{0,32,64,96,128,160,192,224,256,288,320,352,384,416,448,480},{16,48,80,..., dimensions={0} | all-to-all | bytes 1835008 | tf_op jit(solution)/shard_map/all_to_all | solution.py:20
  108.4 0.1 convert_reduce_fusion
  108.5 0.0 copy-done.2
  108.5 0.0 copy-done.3
  108.5 0.8 divide_convert_fusion
  109.3 0.1 broadcast_in_dim.36
  109.3 16.9 %all_to_all.21 = bf16[16,16,1792]{2,1,0:T(8,128)(2,1)S(1)} all-to-all(bf16[16,16,1792]{2,1,0:T(8,128)(2,1)S(1)} %broadcast_in_dim.36), channel_id=1, replica_groups={{0,32,64,96,128,160,192,224,256,288,320,352,384,416,448,480},{16,48,80,..., dimensions={0} | all-to-all | bytes 1835008 | tf_op jit(solution)/shard_map/all_to_all | solution.py:20
  126.3 1.9 %collective-permute-start.5 = (bf16[256,1792]{1,0:T(8,128)(2,1)S(1)}, bf16[256,1792]{1,0:T(8,128)(2,1)S(1)}, u32[]{:S(2)}, u32[]{:S(2)}) collective-permute-start(bf16[256,1792]{1,0:T(8,128)(2,1)S(1)} %bitcast.19), channel_id=1, source_target_pairs={{0,16},{16,0},{32,48},{48,32},{64,80},{80,64},{96,112},{112,96},{1... | collective-permute-start | bytes 2752520 | tf_op jit(solution)/shard_map/ppermute | solution.py:96
  128.2 3.4 %collective-permute-start.4 = (bf16[256,512]{1,0:T(8,128)(2,1)S(1)}, bf16[256,512]{1,0:T(8,128)(2,1)S(1)}, u32[]{:S(2)}, u32[]{:S(2)}) collective-permute-start(bf16[256,512]{1,0:T(8,128)(2,1)S(1)} %constant_dynamic-slice_fusion), channel_id=1, source_target_pairs={{0,0},{1,45},{2,74},{3,103},{4,132},{5,161},{6,206},{7,235},{8,264... | collective-permute-start | bytes 786440 | tf_op jit(solution)/shard_map/ppermute | solution.py:68
  131.7 26.2 %collective-permute-done.4 = bf16[256,512]{1,0:T(8,128)(2,1)S(1)} collective-permute-done((bf16[256,512]{1,0:T(8,128)(2,1)S(1)}, bf16[256,512]{1,0:T(8,128)(2,1)S(1)}, u32[]{:S(2)}, u32[]{:S(2)}) %collective-permute-start.4) | collective-permute-done | bytes 262176 | tf_op jit(solution)/shard_map/ppermute | solution.py:68
  157.9 0.4 convolution_convert_fusion.1
  158.2 0.4 fusion.10
  158.7 0.0 collective-permute-done.5
  158.7 1.3 fusion.1
  (7 shorter events, 0.1 us)
Async XLA Ops:
  0.6 1.0 copy-start
  1.7 27.4 %copy-start.1 = (bf16[512,1792]{1,0:T(8,128)(2,1)S(1)}, bf16[512,1792]{1,0:T(8,128)(2,1)}, u32[]{:S(2)}) copy-start(bf16[512,1792]{1,0:T(8,128)(2,1)} %param.7) | copy-start | bytes 5505028
  1.7 29.3 %copy-start.4 = (s32[4]{0:T(128)S(1)}, s32[4]{0:T(128)}, u32[]{:S(2)}) copy-start(s32[4]{0:T(128)} %param.11) | copy-start | bytes 52
  3.2 10.1 %collective-permute-start = (bf16[256,512]{1,0:T(8,128)(2,1)S(1)}, bf16[256,512]{1,0:T(8,128)(2,1)S(1)}, u32[]{:S(2)}, u32[]{:S(2)}) collective-permute-start(bf16[256,512]{1,0:T(8,128)(2,1)S(1)} %convolution_convert_fusion.2), channel_id=1, source_target_pairs={{0,1},{1,0},{2,3},{3,2},{4,5},{5,4},{6,7},{7,6},{8,9},{9,8},{10,11... | collective-permute-start | bytes 786440 | tf_op jit(solution)/shard_map/ppermute | solution.py:65
  14.1 35.4 %all-to-all-start = ((bf16[8,32,512]{2,1,0:T(8,128)(2,1)}), bf16[8,32,512]{2,1,0:T(8,128)(2,1)S(1)}, u32[]{:S(2)}, u32[]{:S(2)}) async-start(bf16[8,32,512]{2,1,0:T(8,128)(2,1)} %bitcast), calls=%async_computation | async-start | bytes 524288 | tf_op jit(solution)/shard_map/all_to_all | solution.py:20
  29.0 51.1 %collective-permute-start.3 = (bf16[512,1792]{1,0:T(8,128)(2,1)S(1)}, bf16[512,1792]{1,0:T(8,128)(2,1)}, u32[]{:S(2)}, u32[]{:S(2)}) collective-permute-start(bf16[512,1792]{1,0:T(8,128)(2,1)S(1)} %copy-done.1), channel_id=1, source_target_pairs={{0,16},{16,0},{32,48},{48,32},{64,80},{80,64},{96,112},{112,96},{1... | collective-permute-start | bytes 5505032 | tf_op jit(solution)/shard_map/ppermute | solution.py:72
  49.6 3.1 %collective-permute-start.1 = (bf16[16,512]{1,0:T(8,128)(2,1)S(1)}, bf16[16,512]{1,0:T(8,128)(2,1)S(1)}, u32[]{:S(2)}, u32[]{:S(2)}) collective-permute-start(bf16[16,512]{1,0:T(8,128)(2,1)S(1)} %get-tuple-element.9), channel_id=1, source_target_pairs={{0,16},{16,0},{32,48},{48,32},{64,80},{80,64},{96,112},{112,96},{1... | collective-permute-start | bytes 49160 | tf_op jit(solution)/shard_map/ppermute | solution.py:78
  53.4 24.7 %all-to-all-start.1 = ((bf16[8,16,1024]{2,1,0:T(8,128)(2,1)}), bf16[8,16,1024]{2,1,0:T(8,128)(2,1)S(1)}, u32[]{:S(2)}, u32[]{:S(2)}) async-start(bf16[8,16,1024]{2,1,0:T(8,128)(2,1)} %broadcast_in_dim.33), calls=%async_computation.1 | async-start | bytes 524288 | tf_op jit(solution)/shard_map/all_to_all | solution.py:20
  78.1 10.1 %collective-permute-start.2 = (bf16[128,1024]{1,0:T(8,128)(2,1)S(1)}, bf16[128,1024]{1,0:T(8,128)(2,1)S(1)}, u32[]{:S(2)}, u32[]{:S(2)}) collective-permute-start(bf16[128,1024]{1,0:T(8,128)(2,1)S(1)} %bitcast.21), channel_id=1, source_target_pairs={{0,1},{1,0},{2,3},{3,2},{4,5},{5,4},{6,7},{7,6},{8,9},{9,8},{10,11... | collective-permute-start | bytes 786440 | tf_op jit(solution)/shard_map/ppermute | solution.py:81
  89.4 19.1 %copy-start.2 = (f32[16,1792]{1,0:T(8,128)S(1)}, f32[16,1792]{1,0:T(8,128)}, u32[]{:S(2)}) copy-start(f32[16,1792]{1,0:T(8,128)} %param.10) | copy-start | bytes 344068
  89.4 19.1 %copy-start.3 = (f32[16,1792]{1,0:T(8,128)S(1)}, f32[16,1792]{1,0:T(8,128)}, u32[]{:S(2)}) copy-start(f32[16,1792]{1,0:T(8,128)} %param.9) | copy-start | bytes 344068
  126.3 32.4 %collective-permute-start.5 = (bf16[256,1792]{1,0:T(8,128)(2,1)S(1)}, bf16[256,1792]{1,0:T(8,128)(2,1)S(1)}, u32[]{:S(2)}, u32[]{:S(2)}) collective-permute-start(bf16[256,1792]{1,0:T(8,128)(2,1)S(1)} %bitcast.19), channel_id=1, source_target_pairs={{0,16},{16,0},{32,48},{48,32},{64,80},{80,64},{96,112},{112,96},{1... | collective-permute-start | bytes 2752520 | tf_op jit(solution)/shard_map/ppermute | solution.py:96
  128.2 29.7 %collective-permute-start.4 = (bf16[256,512]{1,0:T(8,128)(2,1)S(1)}, bf16[256,512]{1,0:T(8,128)(2,1)S(1)}, u32[]{:S(2)}, u32[]{:S(2)}) collective-permute-start(bf16[256,512]{1,0:T(8,128)(2,1)S(1)} %constant_dynamic-slice_fusion), channel_id=1, source_target_pairs={{0,0},{1,45},{2,74},{3,103},{4,132},{5,161},{6,206},{7,235},{8,264... | collective-permute-start | bytes 786440 | tf_op jit(solution)/shard_map/ppermute | solution.py:68

commit v5 on v4

--- a/solution.py
+++ b/solution.py
@@ -33,7 +33,11 @@
     return scaled.reshape(-1)
 
 
-def basis_routes(chips, splits):
+def reversed_bits(index, bits):
+    return sum(((index >> i) & 1) << (bits - 1 - i) for i in range(bits))
+
+
+def piece_routes(chips, splits):
     return [
         ((2 * k + b) * splits + s, (2 * s + b) * splits + (k - 3 * s) % splits)
         for k in range(chips)
@@ -63,14 +67,24 @@
         return lax.dot_general(part, tokens, (((0,), (1,)), ((), ())), preferred_element_type=f32)
 
     received = lax.ppermute(coordinates_of(1 - parity).astype(bf16), "tensor", neighbor)
+    split = lax.axis_index("tensor")
+    levels = splits.bit_length() - 1
     block_rows = galore_basis.shape[0] * splits // replicas
-    half_block = lax.dynamic_slice_in_dim(galore_basis, core * block_rows, block_rows, 0)
-    local_basis = lax.ppermute(half_block, ("dp", "tensor"), basis_routes(chips, splits))
+    piece_rows = block_rows // splits
+    served = (lax.axis_index("dp") // 2 - 3 * split) % splits
+    start = core * block_rows + reversed_bits(served, levels) * piece_rows
+    local_basis = lax.dynamic_slice_in_dim(galore_basis, start, piece_rows, 0)
+    local_basis = lax.ppermute(local_basis, ("dp", "tensor"), piece_routes(chips, splits))
+    for level in reversed(range(levels)):
+        distance = 1 << level
+        theirs = lax.ppermute(local_basis, "tensor", [(i, i ^ distance) for i in range(splits)])
+        first = (split >> level) % 2 == 0
+        halves = (jnp.where(first, local_basis, theirs), jnp.where(first, theirs, local_basis))
+        local_basis = jnp.concatenate(halves, axis=0)
     kept = lax.optimization_barrier(coordinates_of(parity))
     pair_sum = (kept + received.astype(f32)).astype(bf16)
     arrived = exchange(pair_sum.reshape(splits // 2, rank // splits, slots), "tensor", same_parity)
     partner_grad = lax.ppermute(out_grad, "dp", other_core)
-    both_grads = lax.optimization_barrier(jnp.concatenate([out_grad, partner_grad], axis=0))
     coordinates = arrived.astype(f32).sum(axis=0)
     weighted = (coordinates * token_weights(list_lengths)[None, :]).astype(bf16)
     by_core = weighted.reshape(2, owned, slots)
@@ -82,8 +96,9 @@
     low = jnp.where(parity == 0, near, far)
     high = jnp.where(parity == 0, far, near)
     rows = jnp.concatenate([low, high], axis=0)
-    chip_sum = jnp.dot(rows, both_grads, preferred_element_type=f32).astype(bf16)
-    chip_sum = chip_sum.reshape(chips, owned, columns)
+    kept = jnp.dot(rows[:, :slots], out_grad, preferred_element_type=f32)
+    kept = kept + jnp.dot(rows[:, slots:], partner_grad, preferred_element_type=f32)
+    chip_sum = kept.astype(bf16).reshape(chips, owned, columns)
     gradient = exchange(chip_sum, "dp", same_core).astype(f32).sum(axis=0)
 
     new_first = beta_first * first_moment + (1.0 - beta_first) * gradient

time: 161 us -> 160 us (level)
  the two profiles are of different devices: /device:TPU:26 before, /device:TPU:20 now
where the time goes in v5:
time: 160 us; the launch traced here: 159 us
  starting transfers between devices  65.3 us (41%)
  waiting for transfers between devices  55.5 us (35%)
  blocking collectives  24.2 us (15%)
  matrix products  8.77 us (5%)
  local copies, waits for them, and re-layouts  2.05 us (1%)
  other arithmetic  1.96 us (1%)
    all_to_all x3, starting transfers between devices, exchange(): lax.all_to_all(tiles, axis, split_axis=0, concat_axis=0, tiled=True, axis...  34.8 us
    all_to_all x1, blocking collectives, exchange(): lax.all_to_all(tiles, axis, split_axis=0, concat_axis=0, tiled=True, axis...  24.2 us
    all_to_all x3, waiting for transfers between devices, exchange(): lax.all_to_all(tiles, axis, split_axis=0, concat_axis=0, tiled=True, axis...  18.5 us
    ppermute x4, waiting for transfers between devices, body(): lax.ppermute(local_basis, 'tensor', [(i, i ^ distance) for i in range(spl...  15 us
    ppermute x4, starting transfers between devices, body(): lax.ppermute(local_basis, 'tensor', [(i, i ^ distance) for i in range(spl...  15 us
    ppermute x1, waiting for transfers between devices, body(): lax.ppermute(local_basis, ('dp', 'tensor'), piece_routes(chips, splits))  9.51 us
    ppermute x1, waiting for transfers between devices, body(): far = lax.ppermute(near, 'tensor', neighbor)  6.43 us
    ppermute x1, waiting for transfers between devices, body(): lax.ppermute(coordinates_of(1 - parity).astype(bf16), 'tensor', neighbor)  4.88 us
  transfers between devices with their start and end apart: 13, of which 8 were waited for; matrix products, arithmetic and copies ran while one was open for 3% of the time, Pallas kernels for 0%

profile of v5, /device:TPU:20, one launch (start us, length us, event | category | flops | bytes accessed | tf_op | source)
XLA Modules:
  0.0 158.8 jit_solution(1059789304709934430)
XLA Ops:
  0.6 0.0 copy-start
  0.7 1.0 copy-done
  1.7 0.0 copy-start.1
  1.7 0.0 copy-start.4
  1.7 1.5 convolution_convert_fusion.1
  3.2 3.8 %collective-permute-start = (bf16[256,512]{1,0:T(8,128)(2,1)S(1)}, bf16[256,512]{1,0:T(8,128)(2,1)S(1)}, u32[]{:S(2)}, u32[]{:S(2)}) collective-permute-start(bf16[256,512]{1,0:T(8,128)(2,1)S(1)} %convolution_convert_fusion.1), channel_id=1, source_target_pairs={{0,1},{1,0},{2,3},{3,2},{4,5},{5,4},{6,7},{7,6},{8,9},{9,8},{10,11... | collective-permute-start | bytes 786440 | tf_op jit(solution)/shard_map/ppermute | solution.py:69
  7.1 1.4 fusion.12
  8.5 4.9 %collective-permute-done = bf16[256,512]{1,0:T(8,128)(2,1)S(1)} collective-permute-done((bf16[256,512]{1,0:T(8,128)(2,1)S(1)}, bf16[256,512]{1,0:T(8,128)(2,1)S(1)}, u32[]{:S(2)}, u32[]{:S(2)}) %collective-permute-start) | collective-permute-done | bytes 262176 | tf_op jit(solution)/shard_map/ppermute | solution.py:69
  13.3 0.8 add_convert_fusion
  14.1 14.9 %all-to-all-start = ((bf16[8,32,512]{2,1,0:T(8,128)(2,1)}), bf16[8,32,512]{2,1,0:T(8,128)(2,1)S(1)}, u32[]{:S(2)}, u32[]{:S(2)}) async-start(bf16[8,32,512]{2,1,0:T(8,128)(2,1)} %bitcast), calls=%async_computation | async-start | bytes 524288 | tf_op jit(solution)/shard_map/all_to_all | solution.py:20
  29.0 0.0 copy-done.1
  29.0 1.9 %collective-permute-start.3 = (bf16[512,1792]{1,0:T(8,128)(2,1)S(1)}, bf16[512,1792]{1,0:T(8,128)(2,1)}, u32[]{:S(2)}, u32[]{:S(2)}) collective-permute-start(bf16[512,1792]{1,0:T(8,128)(2,1)S(1)} %copy-done.1), channel_id=1, source_target_pairs={{0,16},{16,0},{32,48},{48,32},{64,80},{80,64},{96,112},{112,96},{1... | collective-permute-start | bytes 5505032 | tf_op jit(solution)/shard_map/ppermute | solution.py:87
  31.0 0.0 copy-done.4
  31.0 0.1 select_bitcast_fusion
  31.1 18.5 %all-to-all-done = bf16[8,32,512]{2,1,0:T(8,128)(2,1)S(1)} async-done(((bf16[8,32,512]{2,1,0:T(8,128)(2,1)}), bf16[8,32,512]{2,1,0:T(8,128)(2,1)S(1)}, u32[]{:S(2)}, u32[]{:S(2)}) %all-to-all-start) | async-done | bytes 262176 | tf_op jit(solution)/shard_map/all_to_all | solution.py:20
  49.6 1.9 %collective-permute-start.1 = (bf16[16,512]{1,0:T(8,128)(2,1)S(1)}, bf16[16,512]{1,0:T(8,128)(2,1)S(1)}, u32[]{:S(2)}, u32[]{:S(2)}) collective-permute-start(bf16[16,512]{1,0:T(8,128)(2,1)S(1)} %get-tuple-element.17), channel_id=1, source_target_pairs={{0,16},{16,0},{32,48},{48,32},{64,80},{80,64},{96,112},{112,96},{1... | collective-permute-start | bytes 49160 | tf_op jit(solution)/shard_map/ppermute | solution.py:92
  51.5 1.1 collective-permute-done.1
  52.7 24.2 %all_to_all.20 = bf16[8,16,1024]{2,1,0:T(8,128)(2,1)S(1)} all-to-all(bf16[8,16,1024]{2,1,0:T(8,128)(2,1)S(1)} %broadcast_in_dim.33), channel_id=1, replica_groups={{0,2,4,6,8,10,12,14},{1,3,5,7,9,11,13,15},{16,18,20,22,24,26,28,30},{17..., dimensions={0} | all-to-all | bytes 524288 | tf_op jit(solution)/shard_map/all_to_all | solution.py:20
  76.9 2.1 %collective-permute-start.2 = (bf16[128,1024]{1,0:T(8,128)(2,1)S(1)}, bf16[128,1024]{1,0:T(8,128)(2,1)S(1)}, u32[]{:S(2)}, u32[]{:S(2)}) collective-permute-start(bf16[128,1024]{1,0:T(8,128)(2,1)S(1)} %bitcast.21), channel_id=1, source_target_pairs={{0,1},{1,0},{2,3},{3,2},{4,5},{5,4},{6,7},{7,6},{8,9},{9,8},{10,11... | collective-permute-start | bytes 786440 | tf_op jit(solution)/shard_map/ppermute | solution.py:95
  79.0 6.4 %collective-permute-done.2 = bf16[128,1024]{1,0:T(8,128)(2,1)S(1)} collective-permute-done((bf16[128,1024]{1,0:T(8,128)(2,1)S(1)}, bf16[128,1024]{1,0:T(8,128)(2,1)S(1)}, u32[]{:S(2)}, u32[]{:S(2)}) %collective-permute-start.2) | collective-permute-done | bytes 262176 | tf_op jit(solution)/shard_map/ppermute | solution.py:95
  85.5 0.1 broadcast_select_fusion.1
  85.5 0.0 collective-permute-done.3
  85.5 2.1 %fusion.6 = f32[256,1792]{1,0:T(8,128)S(1)} fusion(bf16[512,1792]{1,0:T(8,128)(2,1)} %collective-permute-done.3, bf16[128,1024]{1,0:T(8,128)(2,1)S(1)} %get-tuple-element.7, bf16[128,1024]{1,0:T(8,128)(2,1)S(1)} %get-tuple-element.6), kind=kOutput, calls=%fused_computation.16 | convolution fusion | flops 470286336 | bytes 4194304 | tf_op jit(solution)/shard_map/dot_general | solution.py:100
  87.7 1.6 fusion.2
  89.3 0.0 copy-start.2
  89.3 0.0 copy-start.3
  89.3 7.4 %all-to-all-start.2 = ((bf16[16,16,1792]{2,1,0:T(8,128)(2,1)}), bf16[16,16,1792]{2,1,0:T(8,128)(2,1)S(1)}, u32[]{:S(2)}, u32[]{:S(2)}) async-start(bf16[16,16,1792]{2,1,0:T(8,128)(2,1)} %bitcast.6), calls=%async_computation.2 | async-start | bytes 1835008 | tf_op jit(solution)/shard_map/all_to_all | solution.py:20
  96.7 3.9 %collective-permute-start.4 = (bf16[16,512]{1,0:T(8,128)(2,1)S(1)}, bf16[16,512]{1,0:T(8,128)(2,1)S(1)}, u32[]{:S(2)}, u32[]{:S(2)}) collective-permute-start(bf16[16,512]{1,0:T(8,128)(2,1)S(1)} %constant_dynamic-slice_fusion), channel_id=1, source_target_pairs={{0,0},{1,45},{2,74},{3,103},{4,132},{5,161},{6,206},{7,235},{8,264... | collective-permute-start | bytes 49160 | tf_op jit(solution)/shard_map/ppermute | solution.py:77
  100.6 9.5 %collective-permute-done.4 = bf16[16,512]{1,0:T(8,128)(2,1)S(1)} collective-permute-done((bf16[16,512]{1,0:T(8,128)(2,1)S(1)}, bf16[16,512]{1,0:T(8,128)(2,1)S(1)}, u32[]{:S(2)}, u32[]{:S(2)}) %collective-permute-start.4) | collective-permute-done | bytes 16416 | tf_op jit(solution)/shard_map/ppermute | solution.py:77
  110.1 2.4 %collective-permute-start.5 = (bf16[16,512]{1,0:T(8,128)(2,1)S(1)}, bf16[16,512]{1,0:T(8,128)(2,1)S(1)}, u32[]{:S(2)}, u32[]{:S(2)}) collective-permute-start(bf16[16,512]{1,0:T(8,128)(2,1)S(1)} %collective-permute-done.4), channel_id=1, source_target_pairs={{0,8},{1,9},{2,10},{3,11},{4,12},{5,13},{6,14},{7,15},{8,0},{9,1},... | collective-permute-start | bytes 49160 | tf_op jit(solution)/shard_map/ppermute | solution.py:80
  112.5 0.0 all-to-all-done.2
  112.5 0.1 convert_reduce_fusion
  112.6 0.0 copy-done.2
  112.6 0.0 copy-done.3
  112.6 0.7 divide_convert_fusion
  113.4 1.0 broadcast_in_dim.36
  114.4 12.5 %all-to-all-start.3 = ((bf16[16,16,1792]{2,1,0:T(8,128)(2,1)}), bf16[16,16,1792]{2,1,0:T(8,128)(2,1)S(1)}, u32[]{:S(2)}, u32[]{:S(2)}) async-start(bf16[16,16,1792]{2,1,0:T(8,128)(2,1)} %broadcast_in_dim.36), calls=%async_computation.3 | async-start | bytes 1835008 | tf_op jit(solution)/shard_map/all_to_all | solution.py:20
  126.9 0.0 collective-permute-done.5
  126.9 2.8 %collective-permute-start.6 = (bf16[32,512]{1,0:T(8,128)(2,1)S(1)}, bf16[32,512]{1,0:T(8,128)(2,1)S(1)}, u32[]{:S(2)}, u32[]{:S(2)}) collective-permute-start(bf16[32,512]{1,0:T(8,128)(2,1)S(1)} %pad_maximum_fusion.5), channel_id=1, source_target_pairs={{0,4},{1,5},{2,6},{3,7},{4,0},{5,1},{6,2},{7,3},{8,12},{9,13},{10,... | collective-permute-start | bytes 98312 | tf_op jit(solution)/shard_map/ppermute | solution.py:80
  129.8 7.0 %collective-permute-done.6 = bf16[32,512]{1,0:T(8,128)(2,1)S(1)} collective-permute-done((bf16[32,512]{1,0:T(8,128)(2,1)S(1)}, bf16[32,512]{1,0:T(8,128)(2,1)S(1)}, u32[]{:S(2)}, u32[]{:S(2)}) %collective-permute-start.6) | collective-permute-done | bytes 32800 | tf_op jit(solution)/shard_map/ppermute | solution.py:80
  136.8 7.8 %collective-permute-start.7 = (bf16[64,512]{1,0:T(8,128)(2,1)S(1)}, bf16[64,512]{1,0:T(8,128)(2,1)S(1)}, u32[]{:S(2)}, u32[]{:S(2)}) collective-permute-start(bf16[64,512]{1,0:T(8,128)(2,1)S(1)} %pad_maximum_fusion.3), channel_id=1, source_target_pairs={{0,2},{1,3},{2,0},{3,1},{4,6},{5,7},{6,4},{7,5},{8,10},{9,11},{10,... | collective-permute-start | bytes 196616 | tf_op jit(solution)/shard_map/ppermute | solution.py:80
  144.6 2.2 %collective-permute-done.7 = bf16[64,512]{1,0:T(8,128)(2,1)S(1)} collective-permute-done((bf16[64,512]{1,0:T(8,128)(2,1)S(1)}, bf16[64,512]{1,0:T(8,128)(2,1)S(1)}, u32[]{:S(2)}, u32[]{:S(2)}) %collective-permute-start.7) | collective-permute-done | bytes 65568 | tf_op jit(solution)/shard_map/ppermute | solution.py:80
  146.9 0.0 all-to-all-done.3
  146.9 1.9 %collective-permute-start.9 = (bf16[256,1792]{1,0:T(8,128)(2,1)S(1)}, bf16[256,1792]{1,0:T(8,128)(2,1)S(1)}, u32[]{:S(2)}, u32[]{:S(2)}) collective-permute-start(bf16[256,1792]{1,0:T(8,128)(2,1)S(1)} %bitcast.19), channel_id=1, source_target_pairs={{0,16},{16,0},{32,48},{48,32},{64,80},{80,64},{96,112},{112,96},{1... | collective-permute-start | bytes 2752520 | tf_op jit(solution)/shard_map/ppermute | solution.py:111
  148.8 1.9 %collective-permute-start.8 = (bf16[128,512]{1,0:T(8,128)(2,1)S(1)}, bf16[128,512]{1,0:T(8,128)(2,1)S(1)}, u32[]{:S(2)}, u32[]{:S(2)}) collective-permute-start(bf16[128,512]{1,0:T(8,128)(2,1)S(1)} %pad_maximum_fusion.2), channel_id=1, source_target_pairs={{0,1},{1,0},{2,3},{3,2},{4,5},{5,4},{6,7},{7,6},{8,9},{9,8},{10,11... | collective-permute-start | bytes 393224 | tf_op jit(solution)/shard_map/ppermute | solution.py:80
  150.8 5.8 %collective-permute-done.8 = bf16[128,512]{1,0:T(8,128)(2,1)S(1)} collective-permute-done((bf16[128,512]{1,0:T(8,128)(2,1)S(1)}, bf16[128,512]{1,0:T(8,128)(2,1)S(1)}, u32[]{:S(2)}, u32[]{:S(2)}) %collective-permute-start.8) | collective-permute-done | bytes 131104 | tf_op jit(solution)/shard_map/ppermute | solution.py:80
  156.7 0.4 convolution_convert_fusion
  157.1 0.4 fusion.15
  157.5 0.0 collective-permute-done.9
  157.5 1.3 fusion.1
  (15 shorter events, 0.2 us)
Async XLA Ops:
  0.6 1.0 copy-start
  1.7 27.3 %copy-start.1 = (bf16[512,1792]{1,0:T(8,128)(2,1)S(1)}, bf16[512,1792]{1,0:T(8,128)(2,1)}, u32[]{:S(2)}) copy-start(bf16[512,1792]{1,0:T(8,128)(2,1)} %param.7) | copy-start | bytes 5505028
  1.7 29.3 %copy-start.4 = (s32[4]{0:T(128)S(1)}, s32[4]{0:T(128)}, u32[]{:S(2)}) copy-start(s32[4]{0:T(128)} %param.11) | copy-start | bytes 52
  3.2 10.1 %collective-permute-start = (bf16[256,512]{1,0:T(8,128)(2,1)S(1)}, bf16[256,512]{1,0:T(8,128)(2,1)S(1)}, u32[]{:S(2)}, u32[]{:S(2)}) collective-permute-start(bf16[256,512]{1,0:T(8,128)(2,1)S(1)} %convolution_convert_fusion.1), channel_id=1, source_target_pairs={{0,1},{1,0},{2,3},{3,2},{4,5},{5,4},{6,7},{7,6},{8,9},{9,8},{10,11... | collective-permute-start | bytes 786440 | tf_op jit(solution)/shard_map/ppermute | solution.py:69
  14.1 35.4 %all-to-all-start = ((bf16[8,32,512]{2,1,0:T(8,128)(2,1)}), bf16[8,32,512]{2,1,0:T(8,128)(2,1)S(1)}, u32[]{:S(2)}, u32[]{:S(2)}) async-start(bf16[8,32,512]{2,1,0:T(8,128)(2,1)} %bitcast), calls=%async_computation | async-start | bytes 524288 | tf_op jit(solution)/shard_map/all_to_all | solution.py:20
  29.0 56.5 %collective-permute-start.3 = (bf16[512,1792]{1,0:T(8,128)(2,1)S(1)}, bf16[512,1792]{1,0:T(8,128)(2,1)}, u32[]{:S(2)}, u32[]{:S(2)}) collective-permute-start(bf16[512,1792]{1,0:T(8,128)(2,1)S(1)} %copy-done.1), channel_id=1, source_target_pairs={{0,16},{16,0},{32,48},{48,32},{64,80},{80,64},{96,112},{112,96},{1... | collective-permute-start | bytes 5505032 | tf_op jit(solution)/shard_map/ppermute | solution.py:87
  49.6 3.1 %collective-permute-start.1 = (bf16[16,512]{1,0:T(8,128)(2,1)S(1)}, bf16[16,512]{1,0:T(8,128)(2,1)S(1)}, u32[]{:S(2)}, u32[]{:S(2)}) collective-permute-start(bf16[16,512]{1,0:T(8,128)(2,1)S(1)} %get-tuple-element.17), channel_id=1, source_target_pairs={{0,16},{16,0},{32,48},{48,32},{64,80},{80,64},{96,112},{112,96},{1... | collective-permute-start | bytes 49160 | tf_op jit(solution)/shard_map/ppermute | solution.py:92
  76.9 8.5 %collective-permute-start.2 = (bf16[128,1024]{1,0:T(8,128)(2,1)S(1)}, bf16[128,1024]{1,0:T(8,128)(2,1)S(1)}, u32[]{:S(2)}, u32[]{:S(2)}) collective-permute-start(bf16[128,1024]{1,0:T(8,128)(2,1)S(1)} %bitcast.21), channel_id=1, source_target_pairs={{0,1},{1,0},{2,3},{3,2},{4,5},{5,4},{6,7},{7,6},{8,9},{9,8},{10,11... | collective-permute-start | bytes 786440 | tf_op jit(solution)/shard_map/ppermute | solution.py:95
  89.3 23.3 %copy-start.2 = (f32[16,1792]{1,0:T(8,128)S(1)}, f32[16,1792]{1,0:T(8,128)}, u32[]{:S(2)}) copy-start(f32[16,1792]{1,0:T(8,128)} %param.10) | copy-start | bytes 344068
  89.3 23.3 %copy-start.3 = (f32[16,1792]{1,0:T(8,128)S(1)}, f32[16,1792]{1,0:T(8,128)}, u32[]{:S(2)}) copy-start(f32[16,1792]{1,0:T(8,128)} %param.9) | copy-start | bytes 344068
  89.3 23.2 %all-to-all-start.2 = ((bf16[16,16,1792]{2,1,0:T(8,128)(2,1)}), bf16[16,16,1792]{2,1,0:T(8,128)(2,1)S(1)}, u32[]{:S(2)}, u32[]{:S(2)}) async-start(bf16[16,16,1792]{2,1,0:T(8,128)(2,1)} %bitcast.6), calls=%async_computation.2 | async-start | bytes 1835008 | tf_op jit(solution)/shard_map/all_to_all | solution.py:20
  96.7 13.4 %collective-permute-start.4 = (bf16[16,512]{1,0:T(8,128)(2,1)S(1)}, bf16[16,512]{1,0:T(8,128)(2,1)S(1)}, u32[]{:S(2)}, u32[]{:S(2)}) collective-permute-start(bf16[16,512]{1,0:T(8,128)(2,1)S(1)} %constant_dynamic-slice_fusion), channel_id=1, source_target_pairs={{0,0},{1,45},{2,74},{3,103},{4,132},{5,161},{6,206},{7,235},{8,264... | collective-permute-start | bytes 49160 | tf_op jit(solution)/shard_map/ppermute | solution.py:77
  110.1 16.8 %collective-permute-start.5 = (bf16[16,512]{1,0:T(8,128)(2,1)S(1)}, bf16[16,512]{1,0:T(8,128)(2,1)S(1)}, u32[]{:S(2)}, u32[]{:S(2)}) collective-permute-start(bf16[16,512]{1,0:T(8,128)(2,1)S(1)} %collective-permute-done.4), channel_id=1, source_target_pairs={{0,8},{1,9},{2,10},{3,11},{4,12},{5,13},{6,14},{7,15},{8,0},{9,1},... | collective-permute-start | bytes 49160 | tf_op jit(solution)/shard_map/ppermute | solution.py:80
  114.4 32.5 %all-to-all-start.3 = ((bf16[16,16,1792]{2,1,0:T(8,128)(2,1)}), bf16[16,16,1792]{2,1,0:T(8,128)(2,1)S(1)}, u32[]{:S(2)}, u32[]{:S(2)}) async-start(bf16[16,16,1792]{2,1,0:T(8,128)(2,1)} %broadcast_in_dim.36), calls=%async_computation.3 | async-start | bytes 1835008 | tf_op jit(solution)/shard_map/all_to_all | solution.py:20
  126.9 9.8 %collective-permute-start.6 = (bf16[32,512]{1,0:T(8,128)(2,1)S(1)}, bf16[32,512]{1,0:T(8,128)(2,1)S(1)}, u32[]{:S(2)}, u32[]{:S(2)}) collective-permute-start(bf16[32,512]{1,0:T(8,128)(2,1)S(1)} %pad_maximum_fusion.5), channel_id=1, source_target_pairs={{0,4},{1,5},{2,6},{3,7},{4,0},{5,1},{6,2},{7,3},{8,12},{9,13},{10,... | collective-permute-start | bytes 98312 | tf_op jit(solution)/shard_map/ppermute | solution.py:80
  136.8 10.1 %collective-permute-start.7 = (bf16[64,512]{1,0:T(8,128)(2,1)S(1)}, bf16[64,512]{1,0:T(8,128)(2,1)S(1)}, u32[]{:S(2)}, u32[]{:S(2)}) collective-permute-start(bf16[64,512]{1,0:T(8,128)(2,1)S(1)} %pad_maximum_fusion.3), channel_id=1, source_target_pairs={{0,2},{1,3},{2,0},{3,1},{4,6},{5,7},{6,4},{7,5},{8,10},{9,11},{10,... | collective-permute-start | bytes 196616 | tf_op jit(solution)/shard_map/ppermute | solution.py:80
  146.9 10.6 %collective-permute-start.9 = (bf16[256,1792]{1,0:T(8,128)(2,1)S(1)}, bf16[256,1792]{1,0:T(8,128)(2,1)S(1)}, u32[]{:S(2)}, u32[]{:S(2)}) collective-permute-start(bf16[256,1792]{1,0:T(8,128)(2,1)S(1)} %bitcast.19), channel_id=1, source_target_pairs={{0,16},{16,0},{32,48},{48,32},{64,80},{80,64},{96,112},{112,96},{1... | collective-permute-start | bytes 2752520 | tf_op jit(solution)/shard_map/ppermute | solution.py:111
  148.8 7.8 %collective-permute-start.8 = (bf16[128,512]{1,0:T(8,128)(2,1)S(1)}, bf16[128,512]{1,0:T(8,128)(2,1)S(1)}, u32[]{:S(2)}, u32[]{:S(2)}) collective-permute-start(bf16[128,512]{1,0:T(8,128)(2,1)S(1)} %pad_maximum_fusion.2), channel_id=1, source_target_pairs={{0,1},{1,0},{2,3},{3,2},{4,5},{5,4},{6,7},{7,6},{8,9},{9,8},{10,11... | collective-permute-start | bytes 393224 | tf_op jit(solution)/shard_map/ppermute | solution.py:80

commit v6 on v4

--- a/solution.py
+++ b/solution.py
@@ -70,7 +70,6 @@
     pair_sum = (kept + received.astype(f32)).astype(bf16)
     arrived = exchange(pair_sum.reshape(splits // 2, rank // splits, slots), "tensor", same_parity)
     partner_grad = lax.ppermute(out_grad, "dp", other_core)
-    both_grads = lax.optimization_barrier(jnp.concatenate([out_grad, partner_grad], axis=0))
     coordinates = arrived.astype(f32).sum(axis=0)
     weighted = (coordinates * token_weights(list_lengths)[None, :]).astype(bf16)
     by_core = weighted.reshape(2, owned, slots)
@@ -82,8 +81,9 @@
     low = jnp.where(parity == 0, near, far)
     high = jnp.where(parity == 0, far, near)
     rows = jnp.concatenate([low, high], axis=0)
-    chip_sum = jnp.dot(rows, both_grads, preferred_element_type=f32).astype(bf16)
-    chip_sum = chip_sum.reshape(chips, owned, columns)
+    kept = jnp.dot(rows[:, :slots], out_grad, preferred_element_type=f32)
+    kept = kept + jnp.dot(rows[:, slots:], partner_grad, preferred_element_type=f32)
+    chip_sum = kept.astype(bf16).reshape(chips, owned, columns)
     gradient = exchange(chip_sum, "dp", same_core).astype(f32).sum(axis=0)
 
     new_first = beta_first * first_moment + (1.0 - beta_first) * gradient

time: 161 us -> 160 us (level)
  the two profiles are of different devices: /device:TPU:26 before, /device:TPU:85 now
where the time goes in v6:
time: 160 us; the launch traced here: 159 us
  blocking collectives  55.2 us (34%)
  waiting for transfers between devices  55 us (34%)
  starting transfers between devices  37.3 us (23%)
  matrix products  7.84 us (5%)
  other arithmetic  1.85 us (1%)
    all_to_all x3, blocking collectives, exchange(): lax.all_to_all(tiles, axis, split_axis=0, concat_axis=0, tiled=True, axis...  55.2 us
    ppermute x1, waiting for transfers between devices, body(): lax.ppermute(half_block, ('dp', 'tensor'), basis_routes(chips, splits))  30.8 us
    all_to_all x1, starting transfers between devices, exchange(): lax.all_to_all(tiles, axis, split_axis=0, concat_axis=0, tiled=True, axis...  13.8 us
    all_to_all x1, waiting for transfers between devices, exchange(): lax.all_to_all(tiles, axis, split_axis=0, concat_axis=0, tiled=True, axis...  12.2 us
    ppermute x1, waiting for transfers between devices, body(): far = lax.ppermute(near, 'tensor', neighbor)  6.68 us
    ppermute x1, starting transfers between devices, body(): lax.ppermute(lax.dynamic_index_in_dim(by_core, 1 - core, 0, keepdims=Fals...  6.42 us
    ppermute x1, starting transfers between devices, body(): other_rows = lax.ppermute(own_rows, 'dp', other_core)  5.71 us
    ppermute x1, waiting for transfers between devices, body(): lax.ppermute(coordinates_of(1 - parity).astype(bf16), 'tensor', neighbor)  4.49 us
  transfers between devices with their start and end apart: 7, of which 5 were waited for; matrix products, arithmetic and copies ran while one was open for 2% of the time, Pallas kernels for 0%

profile of v6, /device:TPU:85, one launch (start us, length us, event | category | flops | bytes accessed | tf_op | source)
XLA Modules:
  0.0 159.3 jit_solution(2378670922749886586)
XLA Ops:
  0.6 0.0 copy-start
  0.7 1.0 copy-done
  1.7 0.0 copy-start.1
  1.7 0.0 copy-start.4
  1.7 1.5 convolution_convert_fusion.1
  3.2 3.5 %collective-permute-start = (bf16[256,512]{1,0:T(8,128)(2,1)S(1)}, bf16[256,512]{1,0:T(8,128)(2,1)S(1)}, u32[]{:S(2)}, u32[]{:S(2)}) collective-permute-start(bf16[256,512]{1,0:T(8,128)(2,1)S(1)} %convolution_convert_fusion.1), channel_id=1, source_target_pairs={{0,1},{1,0},{2,3},{3,2},{4,5},{5,4},{6,7},{7,6},{8,9},{9,8},{10,11... | collective-permute-start | bytes 786440 | tf_op jit(solution)/shard_map/ppermute | solution.py:65
  6.8 1.4 fusion.9
  8.2 4.5 %collective-permute-done = bf16[256,512]{1,0:T(8,128)(2,1)S(1)} collective-permute-done((bf16[256,512]{1,0:T(8,128)(2,1)S(1)}, bf16[256,512]{1,0:T(8,128)(2,1)S(1)}, u32[]{:S(2)}, u32[]{:S(2)}) %collective-permute-start) | collective-permute-done | bytes 262176 | tf_op jit(solution)/shard_map/ppermute | solution.py:65
  12.7 0.8 add_convert_fusion
  13.4 13.8 %all-to-all-start = ((bf16[8,32,512]{2,1,0:T(8,128)(2,1)}), bf16[8,32,512]{2,1,0:T(8,128)(2,1)S(1)}, u32[]{:S(2)}, u32[]{:S(2)}) async-start(bf16[8,32,512]{2,1,0:T(8,128)(2,1)} %bitcast), calls=%async_computation | async-start | bytes 524288 | tf_op jit(solution)/shard_map/all_to_all | solution.py:20
  27.3 0.0 copy-done.1
  27.3 4.0 %collective-permute-start.3 = (bf16[512,1792]{1,0:T(8,128)(2,1)S(1)}, bf16[512,1792]{1,0:T(8,128)(2,1)}, u32[]{:S(2)}, u32[]{:S(2)}) collective-permute-start(bf16[512,1792]{1,0:T(8,128)(2,1)S(1)} %copy-done.1), channel_id=1, source_target_pairs={{0,16},{16,0},{32,48},{48,32},{64,80},{80,64},{96,112},{112,96},{1... | collective-permute-start | bytes 5505032 | tf_op jit(solution)/shard_map/ppermute | solution.py:72
  31.3 0.0 copy-done.4
  31.3 0.1 select_bitcast_fusion
  31.4 12.2 %all-to-all-done = bf16[8,32,512]{2,1,0:T(8,128)(2,1)S(1)} async-done(((bf16[8,32,512]{2,1,0:T(8,128)(2,1)}), bf16[8,32,512]{2,1,0:T(8,128)(2,1)S(1)}, u32[]{:S(2)}, u32[]{:S(2)}) %all-to-all-start) | async-done | bytes 262176 | tf_op jit(solution)/shard_map/all_to_all | solution.py:20
  43.7 6.4 %collective-permute-start.1 = (bf16[16,512]{1,0:T(8,128)(2,1)S(1)}, bf16[16,512]{1,0:T(8,128)(2,1)S(1)}, u32[]{:S(2)}, u32[]{:S(2)}) collective-permute-start(bf16[16,512]{1,0:T(8,128)(2,1)S(1)} %get-tuple-element.9), channel_id=1, source_target_pairs={{0,16},{16,0},{32,48},{48,32},{64,80},{80,64},{96,112},{112,96},{1... | collective-permute-start | bytes 49160 | tf_op jit(solution)/shard_map/ppermute | solution.py:77
  50.1 0.8 collective-permute-done.1
  51.0 23.5 %all_to_all.20 = bf16[8,16,1024]{2,1,0:T(8,128)(2,1)S(1)} all-to-all(bf16[8,16,1024]{2,1,0:T(8,128)(2,1)S(1)} %broadcast_in_dim.33), channel_id=1, replica_groups={{0,2,4,6,8,10,12,14},{1,3,5,7,9,11,13,15},{16,18,20,22,24,26,28,30},{17..., dimensions={0} | all-to-all | bytes 524288 | tf_op jit(solution)/shard_map/all_to_all | solution.py:20
  74.5 1.9 %collective-permute-start.2 = (bf16[128,1024]{1,0:T(8,128)(2,1)S(1)}, bf16[128,1024]{1,0:T(8,128)(2,1)S(1)}, u32[]{:S(2)}, u32[]{:S(2)}) collective-permute-start(bf16[128,1024]{1,0:T(8,128)(2,1)S(1)} %bitcast.23), channel_id=1, source_target_pairs={{0,1},{1,0},{2,3},{3,2},{4,5},{5,4},{6,7},{7,6},{8,9},{9,8},{10,11... | collective-permute-start | bytes 786440 | tf_op jit(solution)/shard_map/ppermute | solution.py:80
  76.4 6.7 %collective-permute-done.2 = bf16[128,1024]{1,0:T(8,128)(2,1)S(1)} collective-permute-done((bf16[128,1024]{1,0:T(8,128)(2,1)S(1)}, bf16[128,1024]{1,0:T(8,128)(2,1)S(1)}, u32[]{:S(2)}, u32[]{:S(2)}) %collective-permute-start.2) | collective-permute-done | bytes 262176 | tf_op jit(solution)/shard_map/ppermute | solution.py:80
  83.1 0.1 broadcast_select_fusion.1
  83.1 0.0 collective-permute-done.3
  83.2 2.1 %fusion.6 = f32[256,1792]{1,0:T(8,128)S(1)} fusion(bf16[512,1792]{1,0:T(8,128)(2,1)} %collective-permute-done.3, bf16[128,1024]{1,0:T(8,128)(2,1)S(1)} %get-tuple-element.7, bf16[128,1024]{1,0:T(8,128)(2,1)S(1)} %get-tuple-element.6), kind=kOutput, calls=%fused_computation.16 | convolution fusion | flops 470286336 | bytes 4194304 | tf_op jit(solution)/shard_map/dot_general | solution.py:85
  85.3 0.7 fusion.2
  86.0 0.0 copy-start.2
  86.0 0.0 copy-start.3
  86.0 16.0 %all_to_all.21 = bf16[16,16,1792]{2,1,0:T(8,128)(2,1)S(1)} all-to-all(bf16[16,16,1792]{2,1,0:T(8,128)(2,1)S(1)} %bitcast.20), channel_id=1, replica_groups={{0,32,64,96,128,160,192,224,256,288,320,352,384,416,448,480},{16,48,80,..., dimensions={0} | all-to-all | bytes 1835008 | tf_op jit(solution)/shard_map/all_to_all | solution.py:20
  102.1 0.1 convert_reduce_fusion
  102.2 0.0 copy-done.2
  102.2 0.0 copy-done.3
  102.2 0.8 divide_convert_fusion
  103.0 0.1 broadcast_in_dim.36
  103.0 15.6 %all_to_all.22 = bf16[16,16,1792]{2,1,0:T(8,128)(2,1)S(1)} all-to-all(bf16[16,16,1792]{2,1,0:T(8,128)(2,1)S(1)} %broadcast_in_dim.36), channel_id=1, replica_groups={{0,32,64,96,128,160,192,224,256,288,320,352,384,416,448,480},{16,48,80,..., dimensions={0} | all-to-all | bytes 1835008 | tf_op jit(solution)/shard_map/all_to_all | solution.py:20
  118.7 5.7 %collective-permute-start.5 = (bf16[256,1792]{1,0:T(8,128)(2,1)S(1)}, bf16[256,1792]{1,0:T(8,128)(2,1)S(1)}, u32[]{:S(2)}, u32[]{:S(2)}) collective-permute-start(bf16[256,1792]{1,0:T(8,128)(2,1)S(1)} %bitcast.21), channel_id=1, source_target_pairs={{0,16},{16,0},{32,48},{48,32},{64,80},{80,64},{96,112},{112,96},{1... | collective-permute-start | bytes 2752520 | tf_op jit(solution)/shard_map/ppermute | solution.py:96
  124.4 1.9 %collective-permute-start.4 = (bf16[256,512]{1,0:T(8,128)(2,1)S(1)}, bf16[256,512]{1,0:T(8,128)(2,1)S(1)}, u32[]{:S(2)}, u32[]{:S(2)}) collective-permute-start(bf16[256,512]{1,0:T(8,128)(2,1)S(1)} %constant_dynamic-slice_fusion), channel_id=1, source_target_pairs={{0,0},{1,45},{2,74},{3,103},{4,132},{5,161},{6,206},{7,235},{8,264... | collective-permute-start | bytes 786440 | tf_op jit(solution)/shard_map/ppermute | solution.py:68
  126.4 30.8 %collective-permute-done.4 = bf16[256,512]{1,0:T(8,128)(2,1)S(1)} collective-permute-done((bf16[256,512]{1,0:T(8,128)(2,1)S(1)}, bf16[256,512]{1,0:T(8,128)(2,1)S(1)}, u32[]{:S(2)}, u32[]{:S(2)}) %collective-permute-start.4) | collective-permute-done | bytes 262176 | tf_op jit(solution)/shard_map/ppermute | solution.py:68
  157.1 0.4 convolution_convert_fusion
  157.5 0.4 fusion.12
  157.9 0.0 collective-permute-done.5
  157.9 1.3 fusion.1
  (8 shorter events, 0.1 us)
Async XLA Ops:
  0.6 1.0 copy-start
  1.7 25.6 %copy-start.1 = (bf16[512,1792]{1,0:T(8,128)(2,1)S(1)}, bf16[512,1792]{1,0:T(8,128)(2,1)}, u32[]{:S(2)}) copy-start(bf16[512,1792]{1,0:T(8,128)(2,1)} %param.7) | copy-start | bytes 5505028
  1.7 29.6 %copy-start.4 = (s32[4]{0:T(128)S(1)}, s32[4]{0:T(128)}, u32[]{:S(2)}) copy-start(s32[4]{0:T(128)} %param.11) | copy-start | bytes 52
  3.2 9.5 %collective-permute-start = (bf16[256,512]{1,0:T(8,128)(2,1)S(1)}, bf16[256,512]{1,0:T(8,128)(2,1)S(1)}, u32[]{:S(2)}, u32[]{:S(2)}) collective-permute-start(bf16[256,512]{1,0:T(8,128)(2,1)S(1)} %convolution_convert_fusion.1), channel_id=1, source_target_pairs={{0,1},{1,0},{2,3},{3,2},{4,5},{5,4},{6,7},{7,6},{8,9},{9,8},{10,11... | collective-permute-start | bytes 786440 | tf_op jit(solution)/shard_map/ppermute | solution.py:65
  13.4 30.2 %all-to-all-start = ((bf16[8,32,512]{2,1,0:T(8,128)(2,1)}), bf16[8,32,512]{2,1,0:T(8,128)(2,1)S(1)}, u32[]{:S(2)}, u32[]{:S(2)}) async-start(bf16[8,32,512]{2,1,0:T(8,128)(2,1)} %bitcast), calls=%async_computation | async-start | bytes 524288 | tf_op jit(solution)/shard_map/all_to_all | solution.py:20
  27.3 55.9 %collective-permute-start.3 = (bf16[512,1792]{1,0:T(8,128)(2,1)S(1)}, bf16[512,1792]{1,0:T(8,128)(2,1)}, u32[]{:S(2)}, u32[]{:S(2)}) collective-permute-start(bf16[512,1792]{1,0:T(8,128)(2,1)S(1)} %copy-done.1), channel_id=1, source_target_pairs={{0,16},{16,0},{32,48},{48,32},{64,80},{80,64},{96,112},{112,96},{1... | collective-permute-start | bytes 5505032 | tf_op jit(solution)/shard_map/ppermute | solution.py:72
  43.7 7.2 %collective-permute-start.1 = (bf16[16,512]{1,0:T(8,128)(2,1)S(1)}, bf16[16,512]{1,0:T(8,128)(2,1)S(1)}, u32[]{:S(2)}, u32[]{:S(2)}) collective-permute-start(bf16[16,512]{1,0:T(8,128)(2,1)S(1)} %get-tuple-element.9), channel_id=1, source_target_pairs={{0,16},{16,0},{32,48},{48,32},{64,80},{80,64},{96,112},{112,96},{1... | collective-permute-start | bytes 49160 | tf_op jit(solution)/shard_map/ppermute | solution.py:77
  74.5 8.6 %collective-permute-start.2 = (bf16[128,1024]{1,0:T(8,128)(2,1)S(1)}, bf16[128,1024]{1,0:T(8,128)(2,1)S(1)}, u32[]{:S(2)}, u32[]{:S(2)}) collective-permute-start(bf16[128,1024]{1,0:T(8,128)(2,1)S(1)} %bitcast.23), channel_id=1, source_target_pairs={{0,1},{1,0},{2,3},{3,2},{4,5},{5,4},{6,7},{7,6},{8,9},{9,8},{10,11... | collective-permute-start | bytes 786440 | tf_op jit(solution)/shard_map/ppermute | solution.py:80
  86.0 16.2 %copy-start.2 = (f32[16,1792]{1,0:T(8,128)S(1)}, f32[16,1792]{1,0:T(8,128)}, u32[]{:S(2)}) copy-start(f32[16,1792]{1,0:T(8,128)} %param.10) | copy-start | bytes 344068
  86.0 16.2 %copy-start.3 = (f32[16,1792]{1,0:T(8,128)S(1)}, f32[16,1792]{1,0:T(8,128)}, u32[]{:S(2)}) copy-start(f32[16,1792]{1,0:T(8,128)} %param.9) | copy-start | bytes 344068
  118.7 39.3 %collective-permute-start.5 = (bf16[256,1792]{1,0:T(8,128)(2,1)S(1)}, bf16[256,1792]{1,0:T(8,128)(2,1)S(1)}, u32[]{:S(2)}, u32[]{:S(2)}) collective-permute-start(bf16[256,1792]{1,0:T(8,128)(2,1)S(1)} %bitcast.21), channel_id=1, source_target_pairs={{0,16},{16,0},{32,48},{48,32},{64,80},{80,64},{96,112},{112,96},{1... | collective-permute-start | bytes 2752520 | tf_op jit(solution)/shard_map/ppermute | solution.py:96
  124.4 32.7 %collective-permute-start.4 = (bf16[256,512]{1,0:T(8,128)(2,1)S(1)}, bf16[256,512]{1,0:T(8,128)(2,1)S(1)}, u32[]{:S(2)}, u32[]{:S(2)}) collective-permute-start(bf16[256,512]{1,0:T(8,128)(2,1)S(1)} %constant_dynamic-slice_fusion), channel_id=1, source_target_pairs={{0,0},{1,45},{2,74},{3,103},{4,132},{5,161},{6,206},{7,235},{8,264... | collective-permute-start | bytes 786440 | tf_op jit(solution)/shard_map/ppermute | solution.py:68

commit v7 on v6

--- a/solution.py
+++ b/solution.py
@@ -35,7 +35,7 @@
 
 def basis_routes(chips, splits):
     return [
-        ((2 * k + b) * splits + s, (2 * s + b) * splits + (k - 3 * s) % splits)
+        ((2 * k + b) * splits + s, (2 * s + b) * splits + (k - s) % splits)
         for k in range(chips)
         for b in range(2)
         for s in range(splits)
@@ -53,7 +53,8 @@
     owned = rank // replicas
     columns = out_grad.shape[1]
     slots = tokens.shape[0]
-    same_core = [[2 * i + c for i in range(chips)] for c in range(2)]
+    chip_order = [(i % 2) * (chips // 2) + i // 2 for i in range(chips)]
+    same_core = [[2 * chip + c for chip in chip_order] for c in range(2)]
     same_parity = [[2 * i + p for i in range(splits // 2)] for p in range(2)]
     other_core = [(i, i ^ 1) for i in range(replicas)]
     neighbor = [(i, i ^ 1) for i in range(splits)]
@@ -76,11 +77,7 @@
     own = lax.dynamic_index_in_dim(by_core, core, 0, keepdims=False)
     traded = lax.ppermute(lax.dynamic_index_in_dim(by_core, 1 - core, 0, keepdims=False), "dp", other_core)
     both = jnp.concatenate([own, traded], axis=1)
-    near = copies_to_all(both, "tensor", splits // 2, same_parity).reshape(half // 2, 2 * slots)
-    far = lax.ppermute(near, "tensor", neighbor)
-    low = jnp.where(parity == 0, near, far)
-    high = jnp.where(parity == 0, far, near)
-    rows = jnp.concatenate([low, high], axis=0)
+    rows = lax.all_gather(both, "tensor", axis=0, tiled=True)
     kept = jnp.dot(rows[:, :slots], out_grad, preferred_element_type=f32)
     kept = kept + jnp.dot(rows[:, slots:], partner_grad, preferred_element_type=f32)
     chip_sum = kept.astype(bf16).reshape(chips, owned, columns)
@@ -96,7 +93,9 @@
     other_rows = lax.ppermute(own_rows, "dp", other_core)
     place = jnp.arange(rank, dtype=jnp.int32)
     within = place % half
-    source = (within // owned) * (2 * owned) + jnp.where(place < half, core, 1 - core) * owned + within % owned
+    chip = within // owned
+    chip = chip % 2 * (chips // 2) + chip // 2
+    source = chip * (2 * owned) + jnp.where(place < half, core, 1 - core) * owned + within % owned
     pick = (place[:, None] == source[None, :]).astype(bf16)
     ordered = jnp.dot(local_basis, pick, preferred_element_type=f32).astype(bf16)
     expanded = jnp.dot(ordered[:, :half], own_rows, preferred_element_type=f32)

time: 160 us -> 154 us (0.963)
  the two profiles are of different devices: /device:TPU:85 before, /device:TPU:62 now
where the time goes in v7:
time: 154 us; the launch traced here: 153 us
  blocking collectives  61.1 us (40%)
  waiting for transfers between devices  53.2 us (35%)
  starting transfers between devices  28 us (18%)
  matrix products  6.21 us (4%)
  local copies, waits for them, and re-layouts  1.97 us (1%)
  other arithmetic  1.81 us (1%)
    all_to_all x2, blocking collectives, exchange(): lax.all_to_all(tiles, axis, split_axis=0, concat_axis=0, tiled=True, axis...  30.7 us
    all_gather x1, blocking collectives, body(): rows = lax.all_gather(both, 'tensor', axis=0, tiled=True)  30.4 us
    ppermute x1, waiting for transfers between devices, body(): lax.ppermute(half_block, ('dp', 'tensor'), basis_routes(chips, splits))  27.7 us
    all_to_all x1, waiting for transfers between devices, exchange(): lax.all_to_all(tiles, axis, split_axis=0, concat_axis=0, tiled=True, axis...  19.8 us
    all_to_all x1, starting transfers between devices, exchange(): lax.all_to_all(tiles, axis, split_axis=0, concat_axis=0, tiled=True, axis...  14.2 us
    ppermute x1, starting transfers between devices, body(): lax.ppermute(half_block, ('dp', 'tensor'), basis_routes(chips, splits))  6.01 us
    ppermute x1, waiting for transfers between devices, body(): lax.ppermute(coordinates_of(1 - parity).astype(bf16), 'tensor', neighbor)  4.58 us
  transfers between devices with their start and end apart: 6, of which 4 were waited for; matrix products, arithmetic and copies ran while one was open for 2% of the time, Pallas kernels for 0%

profile of v7, /device:TPU:62, one launch (start us, length us, event | category | flops | bytes accessed | tf_op | source)
XLA Modules:
  0.0 153.1 jit_solution(8589949551811542234)
XLA Ops:
  0.6 0.0 copy-start
  0.7 1.0 copy-done
  1.7 0.0 copy-start.4
  1.7 1.4 convolution_convert_fusion.1
  3.1 2.0 %collective-permute-start = (bf16[256,512]{1,0:T(8,128)(2,1)S(1)}, bf16[256,512]{1,0:T(8,128)(2,1)S(1)}, u32[]{:S(2)}, u32[]{:S(2)}) collective-permute-start(bf16[256,512]{1,0:T(8,128)(2,1)S(1)} %convolution_convert_fusion.1), channel_id=1, source_target_pairs={{0,1},{1,0},{2,3},{3,2},{4,5},{5,4},{6,7},{7,6},{8,9},{9,8},{10,11... | collective-permute-start | bytes 786440 | tf_op jit(solution)/shard_map/ppermute | solution.py:66
  5.1 1.9 %collective-permute-start.2 = (bf16[512,1792]{1,0:T(8,128)(2,1)}, bf16[512,1792]{1,0:T(8,128)(2,1)S(1)}, u32[]{:S(2)}, u32[]{:S(2)}) collective-permute-start(bf16[512,1792]{1,0:T(8,128)(2,1)} %param.7), channel_id=1, source_target_pairs={{0,16},{16,0},{32,48},{48,32},{64,80},{80,64},{96,112},{112,96},{1... | collective-permute-start | bytes 5505032 | tf_op jit(solution)/shard_map/ppermute | solution.py:73
  7.1 1.4 fusion.8
  8.4 4.6 %collective-permute-done = bf16[256,512]{1,0:T(8,128)(2,1)S(1)} collective-permute-done((bf16[256,512]{1,0:T(8,128)(2,1)S(1)}, bf16[256,512]{1,0:T(8,128)(2,1)S(1)}, u32[]{:S(2)}, u32[]{:S(2)}) %collective-permute-start) | collective-permute-done | bytes 262176 | tf_op jit(solution)/shard_map/ppermute | solution.py:66
  13.0 0.8 add_convert_fusion
  13.8 14.2 %all-to-all-start = ((bf16[8,32,512]{2,1,0:T(8,128)(2,1)}), bf16[8,32,512]{2,1,0:T(8,128)(2,1)S(1)}, u32[]{:S(2)}, u32[]{:S(2)}) async-start(bf16[8,32,512]{2,1,0:T(8,128)(2,1)} %bitcast), calls=%async_computation | async-start | bytes 524288 | tf_op jit(solution)/shard_map/all_to_all | solution.py:20
  28.0 0.0 copy-done.4
  28.0 0.1 select_bitcast_fusion
  28.1 19.8 %all-to-all-done = bf16[8,32,512]{2,1,0:T(8,128)(2,1)S(1)} async-done(((bf16[8,32,512]{2,1,0:T(8,128)(2,1)}), bf16[8,32,512]{2,1,0:T(8,128)(2,1)S(1)}, u32[]{:S(2)}, u32[]{:S(2)}) %all-to-all-start) | async-done | bytes 262176 | tf_op jit(solution)/shard_map/all_to_all | solution.py:20
  47.9 1.9 %collective-permute-start.1 = (bf16[16,512]{1,0:T(8,128)(2,1)S(1)}, bf16[16,512]{1,0:T(8,128)(2,1)S(1)}, u32[]{:S(2)}, u32[]{:S(2)}) collective-permute-start(bf16[16,512]{1,0:T(8,128)(2,1)S(1)} %get-tuple-element.7), channel_id=1, source_target_pairs={{0,16},{16,0},{32,48},{48,32},{64,80},{80,64},{96,112},{112,96},{1... | collective-permute-start | bytes 49160 | tf_op jit(solution)/shard_map/ppermute | solution.py:78
  49.9 1.1 collective-permute-done.1
  51.0 30.4 %all_gather.3 = bf16[256,1024]{1,0:T(8,128)(2,1)S(1)} all-gather(bf16[16,1024]{1,0:T(8,128)(2,1)S(1)} %pad_maximum_fusion), channel_id=1, replica_groups=mesh['dp'=32,'tensor'=16] {'tensor'}, dimensions={0}, use_global_device_ids=true | all-gather | bytes 557056 | tf_op jit(solution)/shard_map/all_gather | solution.py:80
  81.4 0.0 copy-start.1
  81.4 0.0 collective-permute-done.2
  81.4 0.7 fusion.4
  82.1 0.8 copy-done.1
  82.9 0.6 fusion.2
  83.6 0.0 copy-start.2
  83.6 0.0 copy-start.3
  83.6 15.2 %all_to_all.15 = bf16[16,16,1792]{2,1,0:T(8,128)(2,1)S(1)} all-to-all(bf16[16,16,1792]{2,1,0:T(8,128)(2,1)S(1)} %bitcast.17), channel_id=1, replica_groups={{0,256,32,288,64,320,96,352,128,384,160,416,192,448,224,480},{16,272,48..., dimensions={0} | all-to-all | bytes 1835008 | tf_op jit(solution)/shard_map/all_to_all | solution.py:20
  98.8 0.1 convert_reduce_fusion
  99.0 0.0 copy-done.2
  99.0 0.0 copy-done.3
  99.0 0.8 divide_convert_fusion
  99.7 0.1 broadcast_in_dim.32
  99.8 15.5 %all_to_all.16 = bf16[16,16,1792]{2,1,0:T(8,128)(2,1)S(1)} all-to-all(bf16[16,16,1792]{2,1,0:T(8,128)(2,1)S(1)} %broadcast_in_dim.32), channel_id=1, replica_groups={{0,256,32,288,64,320,96,352,128,384,160,416,192,448,224,480},{16,272,48..., dimensions={0} | all-to-all | bytes 1835008 | tf_op jit(solution)/shard_map/all_to_all | solution.py:20
  115.3 1.9 %collective-permute-start.4 = (bf16[256,1792]{1,0:T(8,128)(2,1)S(1)}, bf16[256,1792]{1,0:T(8,128)(2,1)S(1)}, u32[]{:S(2)}, u32[]{:S(2)}) collective-permute-start(bf16[256,1792]{1,0:T(8,128)(2,1)S(1)} %bitcast.18), channel_id=1, source_target_pairs={{0,16},{16,0},{32,48},{48,32},{64,80},{80,64},{96,112},{112,96},{1... | collective-permute-start | bytes 2752520 | tf_op jit(solution)/shard_map/ppermute | solution.py:93
  117.2 6.0 %collective-permute-start.3 = (bf16[256,512]{1,0:T(8,128)(2,1)S(1)}, bf16[256,512]{1,0:T(8,128)(2,1)S(1)}, u32[]{:S(2)}, u32[]{:S(2)}) collective-permute-start(bf16[256,512]{1,0:T(8,128)(2,1)S(1)} %constant_dynamic-slice_fusion), channel_id=1, source_target_pairs={{0,0},{1,47},{2,78},{3,109},{4,140},{5,171},{6,202},{7,233},{8,264... | collective-permute-start | bytes 786440 | tf_op jit(solution)/shard_map/ppermute | solution.py:69
  123.3 27.7 %collective-permute-done.3 = bf16[256,512]{1,0:T(8,128)(2,1)S(1)} collective-permute-done((bf16[256,512]{1,0:T(8,128)(2,1)S(1)}, bf16[256,512]{1,0:T(8,128)(2,1)S(1)}, u32[]{:S(2)}, u32[]{:S(2)}) %collective-permute-start.3) | collective-permute-done | bytes 262176 | tf_op jit(solution)/shard_map/ppermute | solution.py:69
  151.0 0.4 convolution_convert_fusion
  151.4 0.4 fusion.11
  151.8 0.0 collective-permute-done.4
  151.8 1.3 fusion.1
  (7 shorter events, 0.1 us)
Async XLA Ops:
  0.6 1.0 copy-start
  1.7 26.3 %copy-start.4 = (s32[4]{0:T(128)S(1)}, s32[4]{0:T(128)}, u32[]{:S(2)}) copy-start(s32[4]{0:T(128)} %param.11) | copy-start | bytes 52
  3.1 9.9 %collective-permute-start = (bf16[256,512]{1,0:T(8,128)(2,1)S(1)}, bf16[256,512]{1,0:T(8,128)(2,1)S(1)}, u32[]{:S(2)}, u32[]{:S(2)}) collective-permute-start(bf16[256,512]{1,0:T(8,128)(2,1)S(1)} %convolution_convert_fusion.1), channel_id=1, source_target_pairs={{0,1},{1,0},{2,3},{3,2},{4,5},{5,4},{6,7},{7,6},{8,9},{9,8},{10,11... | collective-permute-start | bytes 786440 | tf_op jit(solution)/shard_map/ppermute | solution.py:66
  5.1 76.3 %collective-permute-start.2 = (bf16[512,1792]{1,0:T(8,128)(2,1)}, bf16[512,1792]{1,0:T(8,128)(2,1)S(1)}, u32[]{:S(2)}, u32[]{:S(2)}) collective-permute-start(bf16[512,1792]{1,0:T(8,128)(2,1)} %param.7), channel_id=1, source_target_pairs={{0,16},{16,0},{32,48},{48,32},{64,80},{80,64},{96,112},{112,96},{1... | collective-permute-start | bytes 5505032 | tf_op jit(solution)/shard_map/ppermute | solution.py:73
  13.8 34.0 %all-to-all-start = ((bf16[8,32,512]{2,1,0:T(8,128)(2,1)}), bf16[8,32,512]{2,1,0:T(8,128)(2,1)S(1)}, u32[]{:S(2)}, u32[]{:S(2)}) async-start(bf16[8,32,512]{2,1,0:T(8,128)(2,1)} %bitcast), calls=%async_computation | async-start | bytes 524288 | tf_op jit(solution)/shard_map/all_to_all | solution.py:20
  47.9 3.1 %collective-permute-start.1 = (bf16[16,512]{1,0:T(8,128)(2,1)S(1)}, bf16[16,512]{1,0:T(8,128)(2,1)S(1)}, u32[]{:S(2)}, u32[]{:S(2)}) collective-permute-start(bf16[16,512]{1,0:T(8,128)(2,1)S(1)} %get-tuple-element.7), channel_id=1, source_target_pairs={{0,16},{16,0},{32,48},{48,32},{64,80},{80,64},{96,112},{112,96},{1... | collective-permute-start | bytes 49160 | tf_op jit(solution)/shard_map/ppermute | solution.py:78
  81.4 1.5 copy-start.1
  83.6 15.4 %copy-start.2 = (f32[16,1792]{1,0:T(8,128)S(1)}, f32[16,1792]{1,0:T(8,128)}, u32[]{:S(2)}) copy-start(f32[16,1792]{1,0:T(8,128)} %param.10) | copy-start | bytes 344068
  83.6 15.4 %copy-start.3 = (f32[16,1792]{1,0:T(8,128)S(1)}, f32[16,1792]{1,0:T(8,128)}, u32[]{:S(2)}) copy-start(f32[16,1792]{1,0:T(8,128)} %param.9) | copy-start | bytes 344068
  115.3 36.5 %collective-permute-start.4 = (bf16[256,1792]{1,0:T(8,128)(2,1)S(1)}, bf16[256,1792]{1,0:T(8,128)(2,1)S(1)}, u32[]{:S(2)}, u32[]{:S(2)}) collective-permute-start(bf16[256,1792]{1,0:T(8,128)(2,1)S(1)} %bitcast.18), channel_id=1, source_target_pairs={{0,16},{16,0},{32,48},{48,32},{64,80},{80,64},{96,112},{112,96},{1... | collective-permute-start | bytes 2752520 | tf_op jit(solution)/shard_map/ppermute | solution.py:93
  117.2 33.8 %collective-permute-start.3 = (bf16[256,512]{1,0:T(8,128)(2,1)S(1)}, bf16[256,512]{1,0:T(8,128)(2,1)S(1)}, u32[]{:S(2)}, u32[]{:S(2)}) collective-permute-start(bf16[256,512]{1,0:T(8,128)(2,1)S(1)} %constant_dynamic-slice_fusion), channel_id=1, source_target_pairs={{0,0},{1,47},{2,78},{3,109},{4,140},{5,171},{6,202},{7,233},{8,264... | collective-permute-start | bytes 786440 | tf_op jit(solution)/shard_map/ppermute | solution.py:69
